TPU v7x, 256 devices: a whole 4x4x8 slice. The times are simulated.
256 devices in a mesh: board: 128 (over y, x, z), hand: 2 (over core).
Axes of the slice: x: 4, y: 4, z: 8, core: 2. Of those that a mesh axis runs over, the one named last changes fastest.
Arguments:
- opp_reach: bfloat16 [8192, 1326], P('board', 'hand'), may hold values from 0.019897461 to 1
- hand_rank: int32 [8192, 1326], P('board'), may hold values from 0 to 1325, as said below
- hand_cards: int32 [1326, 2], replicated, may hold values from 0 to 51, as said below
- pot: float32 [8192], P('board'), may hold values from 1 to 12
- bet_frac: float32 [8192], P('board'), may hold values from 0.25 to 1.5
- trav_reach: float32 [1326], P('hand'), may hold values from 0.02 to 1
Outputs:
- board_values: float32 [8192, 1326], P('board', 'hand')
- hand_values: float32 [1326], P('hand')
- exploitability: float32 [], replicated
Inputs may be any that keep to these rules, and one draw needn't show every extreme that they name: hand_rank[b, i] is the number of hands strictly weaker than hand i on board b; equal ranks tie. `hand_cards`: the rows are the 1326 distinct pairs of two different cards, smaller card first, in an order drawn from the seed.
All inputs are finite; a program needn't handle non-finite values.
Results may differ from a plain program's by a relative error of at most 0.0003.
Values may be sent and summed in bfloat16 or wider, within the bound.
A program may use at most 64 MiB of HBM per device.

v0:
```python
import functools

import jax
import jax.numpy as jnp
from jax import lax
from jax.sharding import Mesh
from jax.sharding import PartitionSpec as P

CARDS = 52
BLOCK = 8
BOARD = ("board_0", "board_1", "board_2")


def in_order(tiles, dim):
    dims = list(tiles.shape[1:])
    dims[dim] *= tiles.shape[0]
    return jnp.moveaxis(tiles, 0, dim).reshape(dims)


def sent_to_all(x, axis):
    copies = jnp.broadcast_to(x, (lax.axis_size(axis), *x.shape))
    return lax.all_to_all(copies, axis, split_axis=0, concat_axis=0, tiled=True)


def collect(x, axis, dim):
    return in_order(sent_to_all(x, axis), dim)


def one_axis_at_a_time(x, axes):
    return functools.reduce(lax.psum, axes, x)


def total_of_pieces(x, axis):
    return lax.all_gather(x, axis).sum(0)


def incidence(hand_cards, card_count):
    card_ids = jnp.arange(card_count, dtype=jnp.int32)
    return (hand_cards[:, 0:1] == card_ids) | (hand_cards[:, 1:2] == card_ids)


def local(opp_reach, hand_rank, hand_cards, pot, bet_frac, trav_reach):
    boards_here, hand_count = hand_rank.shape
    own_count = opp_reach.shape[1]
    block_size = BLOCK
    offset = lax.axis_index("hand") * own_count
    holding = incidence(hand_cards, CARDS).astype(jnp.float32)
    holding_low = holding.astype(jnp.bfloat16)
    column_reach = collect(opp_reach, "hand", 1)
    row_rank = lax.dynamic_slice_in_dim(hand_rank, offset, own_count, 1)
    row_hold = lax.dynamic_slice_in_dim(holding, offset, own_count, 0)
    boards_use = column_reach.shape[0]
    row_count = row_rank.shape[1]
    blocks = boards_use // block_size

    def one_block(carry, block_data):
        row_block, column_block, reach_block = block_data
        above = column_block[:, None, :] < row_block[:, :, None]
        equal = column_block[:, None, :] == row_block[:, :, None]
        levels = jnp.where(above, 2.0, jnp.where(equal, 1.0, 0.0)).astype(jnp.bfloat16)
        weighted = reach_block[:, :, None] * holding_low[None, :, :]
        prefix = jnp.einsum("brh,bhc->brc", levels, weighted, preferred_element_type=jnp.float32)
        blocked = 0.5 * jnp.sum(prefix, axis=2) - jnp.sum(prefix * row_hold[None, :, :], axis=2)
        card_totals = jnp.dot(reach_block, holding_low, preferred_element_type=jnp.float32)
        live_part = 0.5 * jnp.sum(card_totals, axis=1)[:, None] - jnp.dot(
            card_totals, row_hold.T, precision=lax.Precision.HIGHEST
        )
        return (carry, (blocked - live_part, live_part))

    block_inputs = (
        row_rank.reshape(blocks, block_size, row_count),
        hand_rank.reshape(blocks, block_size, -1),
        column_reach.reshape(blocks, block_size, -1),
    )
    unused, (results, live_blocks) = lax.scan(one_block, jnp.zeros((), jnp.int32), block_inputs)
    results = results.reshape(boards_use, row_count)
    live_raw = live_blocks.reshape(boards_use, row_count)
    live_mass = live_raw + opp_reach.astype(jnp.float32)
    half_pot = (0.5 * pot)[:, None]
    call_value = (half_pot + (bet_frac * pot)[:, None]) * results / hand_count
    fold_value = -half_pot * live_mass / hand_count
    board_values = jnp.maximum(call_value, fold_value)
    boards_total = boards_here * lax.axis_size(BOARD)
    hand_part = jnp.sum(board_values, axis=0) / boards_total
    mass_part = jnp.sum(half_pot * live_mass / hand_count, axis=0) / boards_total
    hand_values, opp_mass = (
        one_axis_at_a_time(hand_part, BOARD),
        one_axis_at_a_time(mass_part, BOARD),
    )
    numerator, denominator = (
        total_of_pieces(jnp.sum(trav_reach * hand_values), "hand"),
        total_of_pieces(jnp.sum(trav_reach * opp_mass), "hand"),
    )
    return (board_values, hand_values, numerator / denominator)


def solution(mesh):
    torus = Mesh(
        mesh.devices.reshape(4, 4, 8, mesh.shape["hand"]), ("board_0", "board_1", "board_2", "hand")
    )
    placed = (P(BOARD, "hand"), P(BOARD, None), P(), P(BOARD), P(BOARD), P("hand"))
    return jax.shard_map(
        local,
        mesh=torus,
        in_specs=placed,
        out_specs=(P(BOARD, "hand"), P("hand"), P()),
        check_vma=False,
    )
```

profile of v0, /device:TPU:1, one launch (start us, length us, event | category | flops | bytes accessed | tf_op | source)
XLA Modules:
  0.0 116.2 jit_solution(11494719287197106505)
XLA Ops:
  0.7 1.6 %broadcast_in_dim.34 = bf16[2,64,663]{2,1,0:T(8,128)(2,1)} broadcast(bf16[64,663]{1,0:T(8,128)(2,1)} %param.8), dimensions={1,2} | broadcast | bytes 254592 | tf_op jit(solution)/shard_map/broadcast_in_dim | solution.py:21
  2.3 6.6 %all-to-all-start = ((bf16[2,64,663]{2,1,0:T(8,128)(2,1)}), bf16[2,64,663]{2,1,0:T(8,128)(2,1)S(1)}, u32[]{:S(2)}, u32[]{:S(2)}) async-start(bf16[2,64,663]{2,1,0:T(8,128)(2,1)} %broadcast_in_dim.34), calls=%async_computation | async-start | bytes 393216 | tf_op jit(solution)/shard_map/all_to_all | solution.py:22
  8.9 0.1 dynamic-slice.2
  9.0 0.1 dynamic-slice.3
  9.1 0.1 dynamic-slice_bitcast_fusion.3
  9.2 0.8 all-to-all-done
  10.1 0.2 copy.9
  10.3 0.2 reshape_reshape.3
  10.5 54.6 %while.13 = (s32[]{:T(128)}, f32[8,8,663]{2,1,0:T(8,128)S(1)}, f32[8,8,663]{2,1,0:T(8,128)S(1)}, s32[8,8,1326]{2,1,0:T(8,128)S(1)}, s32[8,8,663]{2,1,0:T(8,128)S...) while((s32[]{:T(128)}, f32[8,8,663]{2,1,0:T(8,128)S(1)}, ...), condition=%wide.region_4.5_spmd.clone, body=%wide.region_0.4_spmd.clone.sunk | while | flops 773100800 | bytes 1029989 | solution.py:75
  10.6 6.2 %fusion.31 = (f32[8,663]{1,0:T(8,128)S(1)}, f32[8,663]{1,0:T(8,128)S(1)}) fusion(f32[663,52]{0,1:T(8,128)S(1)} %get-tuple-element.207, bf16[1326,52]{0,1:T(8,128)(2,1)S(1)} %convert_convert_fusion.3, bf16[8,1326]{1,0:T(8,128)(2,1)S(1)} %dynamic-slice_bitcast_fusion.7, s32[8,663]{1,0:T(8,128)S(1)} %dynamic-slice_bitcast_fusion.8, ...), kind=kOutput, calls=%fused_computation.41.clone.1 | convolution fusion | flops 767976768 | bytes 403104 | tf_op jit(solution)/shard_map/while/body/eval_jaxpr/brh,bhc->brc/dot_general | solution.py:62
  16.8 0.3 fusion.32
  17.1 0.2 bitcast_dynamic-update-slice_fusion.3
  17.4 0.1 convert_convert_fusion.3
  17.5 6.2 %fusion.31 = (f32[8,663]{1,0:T(8,128)S(1)}, f32[8,663]{1,0:T(8,128)S(1)}) fusion(f32[663,52]{0,1:T(8,128)S(1)} %get-tuple-element.207, bf16[1326,52]{0,1:T(8,128)(2,1)S(1)} %convert_convert_fusion.3, bf16[8,1326]{1,0:T(8,128)(2,1)S(1)} %dynamic-slice_bitcast_fusion.7, s32[8,663]{1,0:T(8,128)S(1)} %dynamic-slice_bitcast_fusion.8, ...), kind=kOutput, calls=%fused_computation.41.clone.1 | convolution fusion | flops 767976768 | bytes 403104 | tf_op jit(solution)/shard_map/while/body/eval_jaxpr/brh,bhc->brc/dot_general | solution.py:62
  23.6 0.3 fusion.32
  23.9 0.2 bitcast_dynamic-update-slice_fusion.3
  24.2 0.1 convert_convert_fusion.3
  24.3 6.2 %fusion.31 = (f32[8,663]{1,0:T(8,128)S(1)}, f32[8,663]{1,0:T(8,128)S(1)}) fusion(f32[663,52]{0,1:T(8,128)S(1)} %get-tuple-element.207, bf16[1326,52]{0,1:T(8,128)(2,1)S(1)} %convert_convert_fusion.3, bf16[8,1326]{1,0:T(8,128)(2,1)S(1)} %dynamic-slice_bitcast_fusion.7, s32[8,663]{1,0:T(8,128)S(1)} %dynamic-slice_bitcast_fusion.8, ...), kind=kOutput, calls=%fused_computation.41.clone.1 | convolution fusion | flops 767976768 | bytes 403104 | tf_op jit(solution)/shard_map/while/body/eval_jaxpr/brh,bhc->brc/dot_general | solution.py:62
  30.5 0.3 fusion.32
  30.8 0.2 bitcast_dynamic-update-slice_fusion.3
  31.0 0.1 convert_convert_fusion.3
  31.1 6.2 %fusion.31 = (f32[8,663]{1,0:T(8,128)S(1)}, f32[8,663]{1,0:T(8,128)S(1)}) fusion(f32[663,52]{0,1:T(8,128)S(1)} %get-tuple-element.207, bf16[1326,52]{0,1:T(8,128)(2,1)S(1)} %convert_convert_fusion.3, bf16[8,1326]{1,0:T(8,128)(2,1)S(1)} %dynamic-slice_bitcast_fusion.7, s32[8,663]{1,0:T(8,128)S(1)} %dynamic-slice_bitcast_fusion.8, ...), kind=kOutput, calls=%fused_computation.41.clone.1 | convolution fusion | flops 767976768 | bytes 403104 | tf_op jit(solution)/shard_map/while/body/eval_jaxpr/brh,bhc->brc/dot_general | solution.py:62
  37.3 0.3 fusion.32
  37.6 0.2 bitcast_dynamic-update-slice_fusion.3
  37.9 0.1 convert_convert_fusion.3
  37.9 6.2 %fusion.31 = (f32[8,663]{1,0:T(8,128)S(1)}, f32[8,663]{1,0:T(8,128)S(1)}) fusion(f32[663,52]{0,1:T(8,128)S(1)} %get-tuple-element.207, bf16[1326,52]{0,1:T(8,128)(2,1)S(1)} %convert_convert_fusion.3, bf16[8,1326]{1,0:T(8,128)(2,1)S(1)} %dynamic-slice_bitcast_fusion.7, s32[8,663]{1,0:T(8,128)S(1)} %dynamic-slice_bitcast_fusion.8, ...), kind=kOutput, calls=%fused_computation.41.clone.1 | convolution fusion | flops 767976768 | bytes 403104 | tf_op jit(solution)/shard_map/while/body/eval_jaxpr/brh,bhc->brc/dot_general | solution.py:62
  44.1 0.3 fusion.32
  44.4 0.2 bitcast_dynamic-update-slice_fusion.3
  44.7 6.2 %fusion.31 = (f32[8,663]{1,0:T(8,128)S(1)}, f32[8,663]{1,0:T(8,128)S(1)}) fusion(f32[663,52]{0,1:T(8,128)S(1)} %get-tuple-element.207, bf16[1326,52]{0,1:T(8,128)(2,1)S(1)} %convert_convert_fusion.3, bf16[8,1326]{1,0:T(8,128)(2,1)S(1)} %dynamic-slice_bitcast_fusion.7, s32[8,663]{1,0:T(8,128)S(1)} %dynamic-slice_bitcast_fusion.8, ...), kind=kOutput, calls=%fused_computation.41.clone.1 | convolution fusion | flops 767976768 | bytes 403104 | tf_op jit(solution)/shard_map/while/body/eval_jaxpr/brh,bhc->brc/dot_general | solution.py:62
  50.9 0.3 fusion.32
  51.2 0.2 bitcast_dynamic-update-slice_fusion.3
  51.6 6.2 %fusion.31 = (f32[8,663]{1,0:T(8,128)S(1)}, f32[8,663]{1,0:T(8,128)S(1)}) fusion(f32[663,52]{0,1:T(8,128)S(1)} %get-tuple-element.207, bf16[1326,52]{0,1:T(8,128)(2,1)S(1)} %convert_convert_fusion.3, bf16[8,1326]{1,0:T(8,128)(2,1)S(1)} %dynamic-slice_bitcast_fusion.7, s32[8,663]{1,0:T(8,128)S(1)} %dynamic-slice_bitcast_fusion.8, ...), kind=kOutput, calls=%fused_computation.41.clone.1 | convolution fusion | flops 767976768 | bytes 403104 | tf_op jit(solution)/shard_map/while/body/eval_jaxpr/brh,bhc->brc/dot_general | solution.py:62
  57.7 0.3 fusion.32
  58.0 0.2 bitcast_dynamic-update-slice_fusion.3
  58.4 6.2 %fusion.31 = (f32[8,663]{1,0:T(8,128)S(1)}, f32[8,663]{1,0:T(8,128)S(1)}) fusion(f32[663,52]{0,1:T(8,128)S(1)} %get-tuple-element.207, bf16[1326,52]{0,1:T(8,128)(2,1)S(1)} %convert_convert_fusion.3, bf16[8,1326]{1,0:T(8,128)(2,1)S(1)} %dynamic-slice_bitcast_fusion.7, s32[8,663]{1,0:T(8,128)S(1)} %dynamic-slice_bitcast_fusion.8, ...), kind=kOutput, calls=%fused_computation.41.clone.1 | convolution fusion | flops 767976768 | bytes 403104 | tf_op jit(solution)/shard_map/while/body/eval_jaxpr/brh,bhc->brc/dot_general | solution.py:62
  64.6 0.3 fusion.32
  64.9 0.2 bitcast_dynamic-update-slice_fusion.3
  65.2 0.8 fusion.17
  66.0 7.1 %all-reduce.4 = (f32[663]{0:T(1024)S(1)}, f32[663]{0:T(1024)S(1)}) all-reduce(f32[663]{0:T(1024)S(1)} %get-tuple-element.113, f32[663]{0:T(1024)S(1)} %get-tuple-element.112), channel_id=1, replica_groups=mesh['board_0'=4,'board_1'=4,'board_2'=8,'hand'=2] {'board_0'}, use_global_device_ids=true, to_apply=%region_6.7 | all-reduce | flops 1326 | bytes 10608 | tf_op jit(solution)/shard_map/psum | solution.py:30
  73.1 8.6 %all-reduce.3 = (f32[663]{0:T(1024)S(1)}, f32[663]{0:T(1024)S(1)}) all-reduce(f32[663]{0:T(1024)S(1)} %get-tuple-element.98, f32[663]{0:T(1024)S(1)} %get-tuple-element.99), channel_id=1, replica_groups=mesh['board_0'=4,'board_1'=4,'board_2'=8,'hand'=2] {'board_1'}, use_global_device_ids=true, to_apply=%region_7.8 | all-reduce | flops 1326 | bytes 10608 | tf_op jit(solution)/shard_map/psum | solution.py:30
  81.7 16.5 %all-reduce.2 = (f32[663]{0:T(1024)S(1)}, f32[663]{0:T(1024)S(1)}) all-reduce(f32[663]{0:T(1024)S(1)} %get-tuple-element.96, f32[663]{0:T(1024)S(1)} %get-tuple-element.97), channel_id=1, replica_groups=mesh['board_0'=4,'board_1'=4,'board_2'=8,'hand'=2] {'board_2'}, use_global_device_ids=true, to_apply=%region_8.9 | all-reduce | flops 1326 | bytes 10608 | tf_op jit(solution)/shard_map/psum | solution.py:30
  98.2 0.6 dynamic-slice
  98.8 0.7 multiply_reduce_fusion.2
  99.5 1.3 %dynamic-update-slice.1 = f32[2]{0:T(128)S(1)} dynamic-update-slice(f32[2]{0:T(128)S(1)} %broadcast.33.clone.1, f32[1]{0:T(128)} %bitcast.7, u32[]{:T(128)} %bitcast.6) | dynamic-update-slice | bytes 12
  100.8 1.4 %dynamic-update-slice = f32[2]{0:T(128)S(1)} dynamic-update-slice(f32[2]{0:T(128)S(1)} %broadcast.33.clone, f32[1]{0:T(128)} %bitcast.5, u32[]{:T(128)} %bitcast.6) | dynamic-update-slice | bytes 12
  102.2 10.3 %all-reduce.5 = (f32[2]{0:T(128)S(1)}, f32[2]{0:T(128)S(1)}) all-reduce(f32[2]{0:T(128)S(1)} %dynamic-update-slice, f32[2]{0:T(128)S(1)} %dynamic-update-slice.1), channel_id=1, replica_groups=mesh['board_0'=4,'board_1'=4,'board_2'=8,'hand'=2] {'hand'}, use_global_device_ids=true, to_apply=%add | all-reduce | flops 4 | bytes 32
  112.4 0.6 reduce_sum.83
  113.0 0.7 reduce_sum.86
  (60 shorter events, 0.7 us)
Async XLA Ops:
  0.6 8.3 %copy-start.2 = (s32[1326,2]{0,1:T(2,128)S(1)}, s32[1326,2]{0,1:T(2,128)}, u32[]{:S(2)}) copy-start(s32[1326,2]{0,1:T(2,128)} %param.10) | copy-start | bytes 31828
  0.6 8.5 %copy-start = (s32[64,1326]{1,0:T(8,128)S(1)}, s32[64,1326]{1,0:T(8,128)}, u32[]{:S(2)}) copy-start(s32[64,1326]{1,0:T(8,128)} %param.9) | copy-start | bytes 1018372
  2.3 7.8 %all-to-all-start = ((bf16[2,64,663]{2,1,0:T(8,128)(2,1)}), bf16[2,64,663]{2,1,0:T(8,128)(2,1)S(1)}, u32[]{:S(2)}, u32[]{:S(2)}) async-start(bf16[2,64,663]{2,1,0:T(8,128)(2,1)} %broadcast_in_dim.34), calls=%async_computation | async-start | bytes 393216 | tf_op jit(solution)/shard_map/all_to_all | solution.py:22
  10.5 54.6 %copy-start.5 = (f32[64]{0:T(128)S(1)}, f32[64]{0:T(128)}, u32[]{:S(2)}) copy-start(f32[64]{0:T(128)} %param.11) | copy-start | bytes 772
  10.5 54.6 %copy-start.6 = (f32[64]{0:T(128)S(1)}, f32[64]{0:T(128)}, u32[]{:S(2)}) copy-start(f32[64]{0:T(128)} %param.12) | copy-start | bytes 772
  10.5 54.6 %copy-start.1 = (bf16[64,663]{1,0:T(8,128)(2,1)S(1)}, bf16[64,663]{1,0:T(8,128)(2,1)}, u32[]{:S(2)}) copy-start(bf16[64,663]{1,0:T(8,128)(2,1)} %param.8) | copy-start | bytes 254596
  65.1 33.1 %copy-start.7 = (u32[256]{0:T(256)S(1)}, u32[256]{0:T(256)}, u32[]{:S(2)}) copy-start(u32[256]{0:T(256)} %constant.54) | copy-start | bytes 3076
  65.1 33.7 %copy-start.3 = (f32[663]{0:T(1024)S(1)}, f32[663]{0:T(1024)}, u32[]{:S(2)}) copy-start(f32[663]{0:T(1024)} %param.13) | copy-start | bytes 7960
  98.2 16.9 %copy-start.4 = (f32[663]{0:T(1024)}, f32[663]{0:T(1024)S(1)}, u32[]{:S(2)}) copy-start(f32[663]{0:T(1024)S(1)} %get-tuple-element.94) | copy-start | bytes 7960
where the time goes:
time: 117 us; the launch traced here: 116 us
  matrix products  53.3 us (46%)
  blocking collectives  42.5 us (36%)
  starting transfers between devices  6.62 us (6%)
  local copies, waits for them, and re-layouts  5.87 us (5%)
  between operations  3.32 us (3%)
  other arithmetic  3.3 us (3%)
    dot_general x8, matrix products, one_block(): jnp.einsum('brh,bhc->brc', levels, weighted, preferred_element_type=jnp.f...  49.3 us
    psum x3, blocking collectives, one_axis_at_a_time(): return functools.reduce(lax.psum, axes, x)  32.2 us
    unnamed x1, blocking collectives  10.3 us
    all_to_all x1, starting transfers between devices, sent_to_all(): return lax.all_to_all(copies, axis, split_axis=0, concat_axis=0, tiled=True)  6.62 us
    unnamed x21, local copies, waits for them, and re-layouts  3.3 us
    dot_general x8, matrix products, one_block(): jnp.dot(reach_block, holding_low, preferred_element_type=jnp.float32)  2.36 us
  transfers between devices with their start and end apart: 1, of which 1 were waited for; matrix products, arithmetic and copies ran while one was open for 0% of the time, Pallas kernels for 0%

commit v1 on v0

v1 whole, which is shorter than its diff:
```python
import functools

import jax
import jax.numpy as jnp
from jax import lax
from jax.experimental import pallas as pl
from jax.experimental.pallas import tpu as pltpu
from jax.sharding import Mesh
from jax.sharding import PartitionSpec as P

CARDS = 52
BOARD = ("board_0", "board_1", "board_2")
BF16 = jnp.bfloat16
F32 = jnp.float32

HALF = CARDS // 2
ROWS = 32
HI, LO = 48, 28
SLOT = 32
GROUP = 8
DBLOCK = 4
NT = (((1,), (1,)), ((), ()))


def iota(shape, axis):
    return lax.broadcasted_iota(jnp.int32, shape, axis)


def split2(x):
    high = x.astype(BF16)
    return high, (x - high.astype(F32)).astype(BF16)


def rank_code(rank):
    return (((rank & 127) | 128) << (rank >> 7)).astype(F32).astype(BF16)


def compute_kernel(
    total_boards, hand_count, own_count, me,
    own_ref, other_ref, rank_ref, cards_ref, pot_ref, bet_ref, trav_ref,
    values_ref, part_ref, sums_ref,
    x_ref, p_ref, o_ref, w_ref, g_ref, q_ref, f_ref, a_ref, b_ref, h_ref, t_ref, s_ref, c_ref,
):
    boards, lanes = own_ref.shape
    width = 2 * lanes
    if me is None:
        me = lax.axis_index("hand")

    for half, (reach, at) in enumerate(((own_ref[...], me), (other_ref[...], 1 - me))):
        cols = slice(half * lanes, (half + 1) * lanes)
        rank = rank_ref[at]
        code = rank_code(rank)
        x_ref[0:boards, cols] = reach
        x_ref[boards : 2 * boards, cols] = reach
        x_ref[2 * boards : 3 * boards, cols] = code
        x_ref[3 * boards : 4 * boards, cols] = code
        hi = (rank * 2341) >> 16
        lo = rank - LO * hi
        f_ref[0, :, cols] = hi.astype(F32)
        f_ref[1, :, cols] = lo.astype(F32)
        f_ref[2, :, cols] = reach.astype(F32)
        c_ref[:, cols] = cards_ref[at]

    row16 = iota((16, width), 0).astype(F32).astype(BF16)

    def hot_rows(d, carry):
        low, high = c_ref[0:1, :], c_ref[1:2, :]
        df = d.astype(F32)
        partner = jnp.where(low == df, high, jnp.where(high == df, low, -1.0))
        for q in range(2):
            rel = partner - float(HALF * q)
            rel = jnp.where(rel < float(HALF), rel, -1.0)
            wide = jnp.broadcast_to(rel, (16, width)).astype(BF16)
            for part in range(2):
                hit = wide == row16 + BF16(16 * part)
                p_ref[q, d, 16 * part : 16 * part + 16, :] = jnp.where(hit, BF16(1), BF16(0))
        return carry

    lax.fori_loop(0, CARDS, hot_rows, 0)

    chunk = CARDS // 2
    for q in range(2):

        def to_cards(i, carry):
            rows = p_ref[q, pl.ds(i * chunk, chunk)].reshape(chunk * ROWS, width)
            got = lax.dot_general(rows, x_ref[...], NT, preferred_element_type=F32)
            o_ref[q, pl.ds(i * chunk, chunk)] = got.reshape(chunk, ROWS, 4 * boards)
            return carry

        lax.fori_loop(0, 2, to_cards, 0)

    first = iota((ROWS, 2 * boards), 1) < boards

    def pack(d, carry):
        w_ref[d] = jnp.where(first, o_ref[0, d, :, 0 : 2 * boards], o_ref[1, d, :, 0 : 2 * boards]).astype(BF16)
        g_ref[d] = jnp.where(first, o_ref[0, d, :, 2 * boards :], o_ref[1, d, :, 2 * boards :]).astype(BF16)
        return carry

    lax.fori_loop(0, CARDS, pack, 0)

    for half in range(2):
        rows = slice(16 * half, 16 * half + 16)

        def pairs(i, carry):
            mine = [g_ref[DBLOCK * i + k, rows, :] for k in range(DBLOCK)]
            sums = [None] * DBLOCK
            for e in range(CARDS):
                ge, we = g_ref[e, rows, :], w_ref[e, rows, :].astype(F32)
                for k in range(DBLOCK):
                    sign = lax.clamp(BF16(-1), mine[k] - ge, BF16(1))
                    term = sign.astype(F32) * we
                    sums[k] = term if sums[k] is None else sums[k] + term
            for k in range(DBLOCK):
                q_ref[DBLOCK * i + k, rows, :] = sums[k]
            return carry

        lax.fori_loop(0, CARDS // DBLOCK, pairs, 0)

    lo_row = iota((16, width), 0).astype(F32).astype(BF16)

    def table(g, carry):
        for b in range(GROUP):
            hi = jnp.broadcast_to(f_ref[0, pl.ds(GROUP * g + b, 1), :], (16, width)).astype(BF16)
            lo = jnp.broadcast_to(f_ref[1, pl.ds(GROUP * g + b, 1), :], (16, width)).astype(BF16)
            reach = jnp.broadcast_to(f_ref[2, pl.ds(GROUP * g + b, 1), :], (16, width)).astype(BF16)
            tile, start = 128 * (b % 2), 128 - SLOT // 2 * b
            for part in range(HI // 16):
                hit = hi == lo_row + BF16(16 * part)
                a_ref[HI * b + 16 * part : HI * b + 16 * part + 16, :] = jnp.where(hit, reach, BF16(0))
            for part in range(SLOT // 16):
                at = tile + (start + 16 * part) % 128
                b_ref[at : at + 16, :] = lax.clamp(
                    BF16(-1), lo_row + BF16(16 * part) - lo, BF16(1)
                )
        got = lax.dot_general(a_ref[...], b_ref[...], NT, preferred_element_type=F32)
        h_ref[0 : GROUP * HI, :] = got[:, 0:128]
        h_ref[GROUP * HI :, :] = got[:, 128:256]
        even = iota((GROUP, 128), 0) % 2 == 0
        block = ((iota((GROUP, 128), 1) + SLOT // 2 * iota((GROUP, 128), 0)) % 128) // SLOT
        for t in range(HI // 4):
            row = None
            for k in range(4):
                at = 4 * t + k
                part = jnp.where(
                    even,
                    h_ref[pl.ds(at, GROUP, stride=HI), :],
                    h_ref[pl.ds(at + GROUP * HI, GROUP, stride=HI), :],
                )
                part = pltpu.roll(part, SLOT * k, 1) if k else part
                row = part if row is None else jnp.where(block == k, part, row)
            t_ref[t, pl.ds(GROUP * g, GROUP), :] = pltpu.roll(row, 0, 1, stride=SLOT // 2, stride_axis=0)
        return carry

    lax.fori_loop(0, boards // GROUP, table, 0)

    tiles = HI // 4
    spot = iota((boards, 128), 1) % SLOT == LO
    below = []
    run = jnp.zeros((boards, 128), F32)
    whole = []
    for t in range(tiles):
        mark = jnp.where(spot, t_ref[t], 0.0)
        whole.append(mark)
        below.append(run)
        run = run + mark
    src, dst = iota((256, 128), 0), iota((256, 128), 1)
    at_spot = src % SLOT == LO
    within = (dst // SLOT > (src - 128) // SLOT).astype(F32) - (dst // SLOT < (src - 128) // SLOT).astype(F32)
    spread = jnp.where(at_spot, jnp.where(src < 128, 1.0, within), 0.0).astype(BF16)
    for t in range(tiles):
        outer = below[t] - (run - below[t] - whole[t])
        both = jnp.concatenate([outer, whole[t]], axis=1)
        high, low = split2(both)
        got = jnp.dot(jnp.concatenate([high, low], axis=0), spread, preferred_element_type=F32)
        t_ref[t] = t_ref[t] + got[:boards] + got[boards:]

    def look_up(g, carry):
        rows = pl.ds(pl.multiple_of(GROUP * g, GROUP), GROUP)
        for k in range(lanes // 128):
            cols = slice(128 * k, 128 * k + 128)
            hi = f_ref[0, rows, cols].astype(jnp.int32)
            lo = f_ref[1, rows, cols].astype(jnp.int32)
            tile = hi >> 2
            at = ((hi & 3) << 5) + lo
            found = jnp.zeros((GROUP, 128), F32)
            for t in range(tiles):
                got = jnp.take_along_axis(t_ref[t, rows, :], at, axis=1, mode="promise_in_bounds")
                found = jnp.where(tile == t, got, found)
            s_ref[rows, cols] = found
        return carry

    lax.fori_loop(0, boards // GROUP, look_up, 0)

    shared = jnp.zeros((2 * boards, lanes), F32)
    turned = jnp.transpose(q_ref[...].reshape(CARDS * ROWS, 2 * boards))
    for q in range(2):
        high, low = split2(turned[boards * q : boards * (q + 1)])
        shared = shared + jnp.dot(
            jnp.concatenate([high, low], axis=0),
            p_ref[q, :, :, 0:lanes].reshape(CARDS * ROWS, lanes),
            preferred_element_type=F32,
        )

    card = iota((64, width), 0).astype(F32)
    hold = ((card == c_ref[0:1, :]) | (card == c_ref[1:2, :])).astype(F32).astype(BF16)
    card_totals = lax.dot_general(x_ref[0:boards, :], hold, NT, preferred_element_type=F32)
    high, low = split2(card_totals)
    held = jnp.dot(jnp.concatenate([high, low], axis=0), hold[:, 0:lanes], preferred_element_type=F32)
    live = (
        0.5 * jnp.sum(card_totals, axis=1, keepdims=True)
        - (held[:boards] + held[boards:])
        + own_ref[...].astype(F32)
    )
    margin = s_ref[...] - (shared[:boards] + shared[boards:])
    half_pot = 0.5 * pot_ref[...]
    call_value = ((half_pot + bet_ref[...] * pot_ref[...]) / hand_count) * margin
    stake = (half_pot / hand_count) * live
    values = jnp.maximum(call_value, -stake)
    values_ref[...] = values[:, 0:own_count]
    part = jnp.sum(values, axis=0, keepdims=True) / total_boards
    mass = jnp.sum(stake, axis=0, keepdims=True) / total_boards
    part = jnp.where(iota((1, lanes), 1) < own_count, part, 0.0)
    part_ref[...] = part
    numerator = jnp.sum(part * trav_ref[...], axis=1, keepdims=True)
    denominator = jnp.sum(mass * trav_ref[...], axis=1, keepdims=True)
    sums_ref[...] = jnp.where(iota((1, 128), 1) == 0, numerator, denominator)


def compute(own, other, rank, cards, pot, bet, trav, total_boards, hand_count, own_count, me=None):
    boards, lanes = own.shape
    width = 2 * lanes
    whole = pl.BlockSpec(memory_space=pltpu.VMEM)
    return pl.pallas_call(
        functools.partial(compute_kernel, total_boards, hand_count, own_count, me),
        out_shape=(
            jax.ShapeDtypeStruct((boards, own_count), F32),
            jax.ShapeDtypeStruct((1, lanes), F32),
            jax.ShapeDtypeStruct((1, 128), F32),
        ),
        in_specs=[whole] * 7,
        out_specs=(whole,) * 3,
        scratch_shapes=[
            pltpu.VMEM((4 * boards, width), BF16),
            pltpu.VMEM((2, CARDS, ROWS, width), BF16),
            pltpu.VMEM((2, CARDS, ROWS, 4 * boards), F32),
            pltpu.VMEM((CARDS, ROWS, 2 * boards), BF16),
            pltpu.VMEM((CARDS, ROWS, 2 * boards), BF16),
            pltpu.VMEM((CARDS, ROWS, 2 * boards), F32),
            pltpu.VMEM((3, boards, width), F32),
            pltpu.VMEM((GROUP * HI, width), BF16),
            pltpu.VMEM((GROUP * SLOT, width), BF16),
            pltpu.VMEM((2 * GROUP * HI, 128), F32),
            pltpu.VMEM((HI // 4, boards, 128), F32),
            pltpu.VMEM((boards, lanes), F32),
            pltpu.VMEM((2, width), F32),
        ],
        compiler_params=pltpu.CompilerParams(vmem_limit_bytes=56 * 1024 * 1024),
        cost_estimate=pl.CostEstimate(flops=10**9, bytes_accessed=10**6, transcendentals=0),
    )(own, other, rank, cards, pot, bet, trav)


def local(opp_reach, hand_rank, hand_cards, pot, bet_frac, trav_reach):
    boards, hand_count = hand_rank.shape
    own_count = opp_reach.shape[1]
    lanes = -(-own_count // 128) * 128
    gap = lanes - own_count
    total_boards = boards * lax.axis_size(BOARD)
    own = jnp.pad(opp_reach, ((0, 0), (0, gap)))
    other = lax.ppermute(own, "hand", [(0, 1), (1, 0)])
    rank = jnp.pad(hand_rank.reshape(boards, 2, own_count).transpose(1, 0, 2), ((0, 0), (0, 0), (0, gap)))
    cards = jnp.pad(
        hand_cards.reshape(2, own_count, 2).transpose(0, 2, 1).astype(F32),
        ((0, 0), (0, 0), (0, gap)),
        constant_values=-1.0,
    )
    trav = jnp.pad(trav_reach, (0, gap))[None, :]
    board_values, part, sums = compute(
        own, other, rank, cards, pot[:, None], bet_frac[:, None], trav, total_boards, hand_count, own_count
    )
    packed = jnp.concatenate([part, sums], axis=1)
    packed = functools.reduce(lax.psum, BOARD, packed)
    hand_values = packed[0, :own_count]
    ends = lax.psum(packed[0, lanes : lanes + 2], "hand")
    return board_values, hand_values, ends[0] / ends[1]


def solution(mesh):
    torus = Mesh(
        mesh.devices.reshape(4, 4, 8, mesh.shape["hand"]), ("board_0", "board_1", "board_2", "hand")
    )
    placed = (P(BOARD, "hand"), P(BOARD, None), P(), P(BOARD), P(BOARD), P("hand"))
    return jax.shard_map(
        local,
        mesh=torus,
        in_specs=placed,
        out_specs=(P(BOARD, "hand"), P("hand"), P()),
        check_vma=False,
    )
```

time: 117 us -> 83.1 us (0.71)
  matrix products: 53.3 us -> 0 us
  Pallas kernels: 0 us -> 24.3 us
  local copies, waits for them, and re-layouts: 5.87 us -> 10.2 us
  starting transfers between devices: 6.62 us -> 3.29 us
  other arithmetic: 3.3 us -> 0.01 us
    dot_general x24 -> x0, matrix products: 53.3 us -> none  [the longest x8 49.3 us: one_block(): jnp.einsum('brh,bhc->brc', levels, weighted, preferred_element_type=jnp.f...]
    pallas_call x0 -> x1, Pallas kernels: none -> 24.3 us  [compute(): pl.pallas_call(functools.partial(compute_kernel, total_boards, hand_count...]
    unnamed x1 -> x0, blocking collectives: 10.3 us -> none
    psum x3 -> x4, blocking collectives: 32.2 us -> 41.6 us  [the longest x3 31.9 us: local(): packed = functools.reduce(lax.psum, BOARD, packed)]
    all_to_all x1 -> x0, starting transfers between devices: 6.62 us -> none  [sent_to_all(): return lax.all_to_all(copies, axis, split_axis=0, concat_axis=0, tiled=True)]
    ppermute x0 -> x1, starting transfers between devices: none -> 3.29 us  [local(): other = lax.ppermute(own, 'hand', [(0, 1), (1, 0)])]
    reduce_sum x4 -> x0, other arithmetic: 2.78 us -> none  [the longest x2 1.28 us: total_of_pieces(): return lax.all_gather(x, axis).sum(0)]
    pad x0 -> x4, local copies, waits for them, and re-layouts: none -> 2.27 us  [the longest x1 0.91 us: local(): own = jnp.pad(opp_reach, ((0, 0), (0, gap)))]
  transfers between devices with their start and end apart: 1 -> 1, of which waited for: 1 -> 0; matrix products, arithmetic and copies ran while one was open for 0% -> 6% of each run, Pallas kernels for 0% -> 0%
where the time goes in v1:
time: 83.1 us; the launch traced here: 82.7 us
  blocking collectives  41.6 us (50%)
  Pallas kernels  24.3 us (29%)
  local copies, waits for them, and re-layouts  10.2 us (12%)
  starting transfers between devices  3.29 us (4%)
  between operations  3.22 us (4%)
    psum x3, blocking collectives, local(): packed = functools.reduce(lax.psum, BOARD, packed)  31.9 us
    pallas_call x1, Pallas kernels, compute(): pl.pallas_call(functools.partial(compute_kernel, total_boards, hand_count...  24.3 us
    psum x1, blocking collectives, local(): ends = lax.psum(packed[0, lanes:lanes + 2], 'hand')  9.76 us
    unnamed x16, local copies, waits for them, and re-layouts  3.29 us
    ppermute x1, starting transfers between devices, local(): other = lax.ppermute(own, 'hand', [(0, 1), (1, 0)])  3.29 us
  transfers between devices with their start and end apart: 1, of which 0 were waited for; matrix products, arithmetic and copies ran while one was open for 6% of the time, Pallas kernels for 0%

profile of v1, /device:TPU:1, one launch (start us, length us, event | category | flops | bytes accessed | tf_op | source)
XLA Modules:
  0.0 82.7 jit_solution(13035844695051317371)
XLA Ops:
  0.6 0.9 %pad.16.own_ref = bf16[64,768]{1,0:T(8,128)(2,1)S(1)} pad(bf16[64,663]{1,0:T(8,128)(2,1)} %param.6, bf16[]{:T(256)} %constant.4.clone.1), padding=0_0x0_105 | pad | bytes 183170 | tf_op jit(solution)/shard_map/jit(_pad)/pad | solution.py:268
  1.5 0.0 copy-start
  1.5 3.3 %collective-permute-start = (bf16[64,768]{1,0:T(8,128)(2,1)S(1)}, bf16[64,768]{1,0:T(8,128)(2,1)S(1)}, u32[]{:S(2)}, u32[]{:S(2)}) collective-permute-start(bf16[64,768]{1,0:T(8,128)(2,1)S(1)} %pad.16.own_ref), channel_id=1, source_target_pairs={{0,1},{1,0},{2,3},{3,2},{4,5},{5,4},{6,7},{7,6},{8,9},{9,8},{10,11... | collective-permute-start | bytes 294920 | tf_op jit(solution)/shard_map/ppermute | solution.py:269
  4.8 1.4 %reshape.12 = s32[64,2,663]{2,1,0:T(2,128)S(1)} reshape(s32[64,1326]{1,0:T(8,128)} %param.7) | data formatting | bytes 678912 | tf_op jit(solution)/shard_map/reshape | solution.py:270
  6.2 0.0 copy-done
  6.2 0.0 copy-start.1
  6.3 0.7 copy-done.1
  6.9 0.1 convert_element_type.14
  7.0 0.0 copy-start.4
  7.0 0.6 copy-done.4
  7.7 0.7 copy.13.pot_ref
  8.4 0.0 copy-start.5
  8.4 0.7 copy-done.5
  9.0 0.0 copy-start.2
  9.0 0.7 copy.14.bet_ref
  9.7 0.0 copy-done.2
  9.7 0.6 broadcast_in_dim.11.trav_ref
  10.3 0.8 pad.17.rank_ref
  11.1 0.6 pad.18.cards_ref
  11.7 0.0 collective-permute-done.other_ref
  11.7 0.0 copy-start.7
  11.7 0.6 copy-done.7
  12.3 24.3 %shard_map.85 = (f32[64,663]{1,0:T(8,128)}, f32[1,768]{1,0:T(1,128)}, f32[1,128]{1,0:T(1,128)}) custom-call(bf16[64,768]{1,0:T(8,128)(2,1)} %copy-done, bf16[64,768]{1,0:T(8,128)(2,1)} %copy-done.7, s32[2,64,768]{2,1,0:T(8,128)} %pad.17.rank_ref, f32[2,2,768]{2,1,0:T(2,128)} %pad.18.cards_ref, f32[64,1]{1,0:T(8,128)} %copy.13.pot_ref, ...), custom_call_target="tpu_custom_call" | custom-call | flops 1000000000 | bytes 1000000 | tf_op jit(solution)/shard_map/pallas_call | solution.py:233
  36.7 0.0 copy-start.3
  36.7 0.0 copy-start.6
  36.7 0.7 copy-done.3
  37.4 0.0 copy-done.6
  37.4 7.0 %psum.28 = f32[1,896]{1,0:T(1,128)S(1)} all-reduce(f32[1,896]{1,0:T(1,128)S(1)} %pad_maximum_fusion), channel_id=1, replica_groups=mesh['board_0'=4,'board_1'=4,'board_2'=8,'hand'=2] {'board_0'}, use_global_device_ids=true, to_apply=%region_0.1 | all-reduce | flops 896 | bytes 7168 | tf_op jit(solution)/shard_map/psum | solution.py:281
  44.4 8.5 %psum.29 = f32[1,896]{1,0:T(1,128)S(1)} all-reduce(f32[1,896]{1,0:T(1,128)S(1)} %psum.28), channel_id=1, replica_groups=mesh['board_0'=4,'board_1'=4,'board_2'=8,'hand'=2] {'board_1'}, use_global_device_ids=true, to_apply=%region_1.2 | all-reduce | flops 896 | bytes 7168 | tf_op jit(solution)/shard_map/psum | solution.py:281
  52.9 16.4 %psum.30 = f32[1,896]{1,0:T(1,128)S(1)} all-reduce(f32[1,896]{1,0:T(1,128)S(1)} %psum.29), channel_id=1, replica_groups=mesh['board_0'=4,'board_1'=4,'board_2'=8,'hand'=2] {'board_2'}, use_global_device_ids=true, to_apply=%region_2.3 | all-reduce | flops 896 | bytes 7168 | tf_op jit(solution)/shard_map/psum | solution.py:281
  69.2 0.6 slice_reduce_fusion
  69.8 9.8 %psum.31 = f32[2]{0:T(128)S(1)} all-reduce(f32[2]{0:T(128)S(1)} %slice_bitcast_fusion), channel_id=1, replica_groups=mesh['board_0'=4,'board_1'=4,'board_2'=8,'hand'=2] {'hand'}, use_global_device_ids=true, to_apply=%region_3.4 | all-reduce | flops 2 | bytes 16 | tf_op jit(solution)/shard_map/psum | solution.py:283
  79.6 0.6 fusion
  (6 shorter events, 0.1 us)
Async XLA Ops:
  1.5 4.7 %copy-start = (bf16[64,768]{1,0:T(8,128)(2,1)}, bf16[64,768]{1,0:T(8,128)(2,1)S(1)}, u32[]{:S(2)}) copy-start(bf16[64,768]{1,0:T(8,128)(2,1)S(1)} %pad.16.own_ref) | copy-start | bytes 294916
  1.5 10.1 %collective-permute-start = (bf16[64,768]{1,0:T(8,128)(2,1)S(1)}, bf16[64,768]{1,0:T(8,128)(2,1)S(1)}, u32[]{:S(2)}, u32[]{:S(2)}) collective-permute-start(bf16[64,768]{1,0:T(8,128)(2,1)S(1)} %pad.16.own_ref), channel_id=1, source_target_pairs={{0,1},{1,0},{2,3},{3,2},{4,5},{5,4},{6,7},{7,6},{8,9},{9,8},{10,11... | collective-permute-start | bytes 294920 | tf_op jit(solution)/shard_map/ppermute | solution.py:269
  6.2 0.7 copy-start.1
  7.0 0.7 copy-start.4
  8.4 0.7 copy-start.5
  9.0 0.7 copy-start.2
  11.7 0.6 copy-start.7
  36.7 0.7 copy-start.3
  36.7 0.7 copy-start.6

commit v2 on v1

--- a/solution.py
+++ b/solution.py
@@ -19,6 +19,8 @@
 SLOT = 32
 GROUP = 8
 DBLOCK = 4
+YS, XS, ZS = 4, 4, 8
+MESH = pl.DeviceIdType.MESH
 NT = (((1,), (1,)), ((), ()))
 
 
@@ -35,59 +37,110 @@
     return (((rank & 127) | 128) << (rank >> 7)).astype(F32).astype(BF16)
 
 
-def compute_kernel(
-    total_boards, hand_count, own_count, me,
-    own_ref, other_ref, rank_ref, cards_ref, pot_ref, bet_ref, trav_ref,
-    values_ref, part_ref, sums_ref,
+def every_peer(places):
+    y, x, z, h = places
+    plane = [
+        {"board_0": lax.rem(y + i, YS), "board_1": lax.rem(x + j, XS)}
+        for i in range(YS)
+        for j in range(XS)
+        if i or j
+    ]
+    line = [{"board_2": lax.rem(z + i, ZS)} for i in range(1, ZS)]
+    cross = [{"board_2": lax.rem(z + i, ZS), "hand": 1 - h} for i in range(ZS)]
+    return plane, line, cross
+
+
+def column(row):
+    n = row.shape[1]
+    return jnp.sum(jnp.where(iota((n, n), 0) == iota((n, n), 1), row, 0.0), axis=1, keepdims=True)
+
+
+def fused_kernel(
+    total_boards, hand_count,
+    reach_ref, rank_ref, cards_ref, pot_ref, bet_ref, trav_ref,
+    values_ref, hand_ref, ratio_ref,
     x_ref, p_ref, o_ref, w_ref, g_ref, q_ref, f_ref, a_ref, b_ref, h_ref, t_ref, s_ref, c_ref,
+    swap_ref, mine_ref, plane_ref, line_ref, cross_ref, swap_sem, plane_sem, line_sem, cross_sem,
 ):
-    boards, lanes = own_ref.shape
+    boards, own_count = reach_ref.shape
+    lanes = x_ref.shape[1] // 2
     width = 2 * lanes
-    if me is None:
-        me = lax.axis_index("hand")
-
-    for half, (reach, at) in enumerate(((own_ref[...], me), (other_ref[...], 1 - me))):
-        cols = slice(half * lanes, (half + 1) * lanes)
-        rank = rank_ref[at]
-        code = rank_code(rank)
-        x_ref[0:boards, cols] = reach
-        x_ref[boards : 2 * boards, cols] = reach
-        x_ref[2 * boards : 3 * boards, cols] = code
-        x_ref[3 * boards : 4 * boards, cols] = code
+    places = tuple(lax.axis_index(name) for name in BOARD) + (lax.axis_index("hand"),)
+    y, x, z, me = places
+    plane, line, cross = every_peer(places)
+    barrier = pltpu.get_barrier_semaphore()
+    for peer in plane + line + cross:
+        pl.semaphore_signal(barrier, inc=1, device_id=peer, device_id_type=MESH)
+
+    def cols_of(half, start=0, size=lanes):
+        return pl.ds(pl.multiple_of(half * lanes + start, 128), size)
+
+    x_ref[0:boards, cols_of(me, lanes - 128, 128)] = jnp.zeros((boards, 128), BF16)
+    x_ref[0:boards, cols_of(1 - me, lanes - 128, 128)] = jnp.zeros((boards, 128), BF16)
+    for half in range(2):
+        start = half * lanes
+        f_ref[0:2, :, start + lanes - 128 : start + lanes] = jnp.zeros((2, boards, 128), F32)
+        x_ref[2 * boards : 3 * boards, start + lanes - 128 : start + lanes] = jnp.zeros((boards, 128), BF16)
+        c_ref[:, start + lanes - 128 : start + lanes] = jnp.full((2, 128), -1.0, F32)
+        c_ref[:, start : start + own_count] = cards_ref[:, half * own_count : (half + 1) * own_count].astype(F32)
+        rank = rank_ref[:, half * own_count : (half + 1) * own_count]
+        x_ref[2 * boards : 3 * boards, start : start + own_count] = rank_code(rank)
         hi = (rank * 2341) >> 16
-        lo = rank - LO * hi
-        f_ref[0, :, cols] = hi.astype(F32)
-        f_ref[1, :, cols] = lo.astype(F32)
-        f_ref[2, :, cols] = reach.astype(F32)
-        c_ref[:, cols] = cards_ref[at]
-
-    row16 = iota((16, width), 0).astype(F32).astype(BF16)
-
-    def hot_rows(d, carry):
-        low, high = c_ref[0:1, :], c_ref[1:2, :]
-        df = d.astype(F32)
-        partner = jnp.where(low == df, high, jnp.where(high == df, low, -1.0))
+        f_ref[0, :, start : start + own_count] = hi.astype(F32)
+        f_ref[1, :, start : start + own_count] = (rank - LO * hi).astype(F32)
+    x_ref[3 * boards : 4 * boards, :] = x_ref[2 * boards : 3 * boards, :]
+
+    def place(half, ref):
+        x_ref[0:boards, pl.ds(pl.multiple_of(half * lanes, 128), own_count)] = ref[...]
+        x_ref[boards : 2 * boards, cols_of(half)] = x_ref[0:boards, cols_of(half)]
+
+    row16 = iota((16, lanes), 0).astype(F32).astype(BF16)
+
+    def hot_rows(half):
+        def one(d, carry):
+            low, high = c_ref[0:1, cols_of(half)], c_ref[1:2, cols_of(half)]
+            df = d.astype(F32)
+            partner = jnp.where(low == df, high, jnp.where(high == df, low, -1.0))
+            for q in range(2):
+                rel = partner - float(HALF * q)
+                rel = jnp.where(rel < float(HALF), rel, -1.0)
+                wide = jnp.broadcast_to(rel, (16, lanes)).astype(BF16)
+                for part in range(2):
+                    hit = wide == row16 + BF16(16 * part)
+                    p_ref[q, d, 16 * part : 16 * part + 16, cols_of(half)] = jnp.where(hit, BF16(1), BF16(0))
+            return carry
+
+        lax.fori_loop(0, CARDS, one, 0)
+
+    chunk = CARDS // 2
+
+    def to_cards(half, more):
         for q in range(2):
-            rel = partner - float(HALF * q)
-            rel = jnp.where(rel < float(HALF), rel, -1.0)
-            wide = jnp.broadcast_to(rel, (16, width)).astype(BF16)
-            for part in range(2):
-                hit = wide == row16 + BF16(16 * part)
-                p_ref[q, d, 16 * part : 16 * part + 16, :] = jnp.where(hit, BF16(1), BF16(0))
-        return carry
-
-    lax.fori_loop(0, CARDS, hot_rows, 0)
-
-    chunk = CARDS // 2
-    for q in range(2):
-
-        def to_cards(i, carry):
-            rows = p_ref[q, pl.ds(i * chunk, chunk)].reshape(chunk * ROWS, width)
-            got = lax.dot_general(rows, x_ref[...], NT, preferred_element_type=F32)
-            o_ref[q, pl.ds(i * chunk, chunk)] = got.reshape(chunk, ROWS, 4 * boards)
-            return carry
-
-        lax.fori_loop(0, 2, to_cards, 0)
+
+            def one(i, carry):
+                rows = p_ref[q, pl.ds(i * chunk, chunk), :, cols_of(half)].reshape(chunk * ROWS, lanes)
+                got = lax.dot_general(rows, x_ref[:, cols_of(half)], NT, preferred_element_type=F32)
+                got = got.reshape(chunk, ROWS, 4 * boards)
+                if more:
+                    got = got + o_ref[q, pl.ds(i * chunk, chunk)]
+                o_ref[q, pl.ds(i * chunk, chunk)] = got
+                return carry
+
+            lax.fori_loop(0, 2, one, 0)
+
+    place(me, reach_ref)
+    hot_rows(me)
+    to_cards(me, False)
+    pl.semaphore_wait(barrier, len(plane + line + cross))
+    swap = pltpu.make_async_remote_copy(
+        reach_ref, swap_ref, swap_sem.at[0], swap_sem.at[1], device_id={"hand": 1 - me}, device_id_type=MESH
+    )
+    swap.start()
+    hot_rows(1 - me)
+    swap.wait()
+    place(1 - me, swap_ref)
+    to_cards(1 - me, True)
+    f_ref[2] = x_ref[0:boards, :].astype(F32)
 
     first = iota((ROWS, 2 * boards), 1) < boards
 
@@ -178,8 +231,8 @@
         rows = pl.ds(pl.multiple_of(GROUP * g, GROUP), GROUP)
         for k in range(lanes // 128):
             cols = slice(128 * k, 128 * k + 128)
-            hi = f_ref[0, rows, cols].astype(jnp.int32)
-            lo = f_ref[1, rows, cols].astype(jnp.int32)
+            hi = f_ref[0, rows, cols_of(me, 128 * k, 128)].astype(jnp.int32)
+            lo = f_ref[1, rows, cols_of(me, 128 * k, 128)].astype(jnp.int32)
             tile = hi >> 2
             at = ((hi & 3) << 5) + lo
             found = jnp.zeros((GROUP, 128), F32)
@@ -197,47 +250,95 @@
         high, low = split2(turned[boards * q : boards * (q + 1)])
         shared = shared + jnp.dot(
             jnp.concatenate([high, low], axis=0),
-            p_ref[q, :, :, 0:lanes].reshape(CARDS * ROWS, lanes),
+            p_ref[q, :, :, cols_of(me)].reshape(CARDS * ROWS, lanes),
             preferred_element_type=F32,
         )
 
-    card = iota((64, width), 0).astype(F32)
-    hold = ((card == c_ref[0:1, :]) | (card == c_ref[1:2, :])).astype(F32).astype(BF16)
-    card_totals = lax.dot_general(x_ref[0:boards, :], hold, NT, preferred_element_type=F32)
+    card = iota((64, lanes), 0).astype(F32)
+    card_totals = jnp.zeros((boards, 64), F32)
+    for half in (1 - me, me):
+        hold = ((card == c_ref[0:1, cols_of(half)]) | (card == c_ref[1:2, cols_of(half)])).astype(F32).astype(BF16)
+        card_totals = card_totals + lax.dot_general(
+            x_ref[0:boards, cols_of(half)], hold, NT, preferred_element_type=F32
+        )
     high, low = split2(card_totals)
-    held = jnp.dot(jnp.concatenate([high, low], axis=0), hold[:, 0:lanes], preferred_element_type=F32)
+    held = jnp.dot(jnp.concatenate([high, low], axis=0), hold, preferred_element_type=F32)
     live = (
         0.5 * jnp.sum(card_totals, axis=1, keepdims=True)
         - (held[:boards] + held[boards:])
-        + own_ref[...].astype(F32)
+        + f_ref[2, :, cols_of(me)]
     )
     margin = s_ref[...] - (shared[:boards] + shared[boards:])
-    half_pot = 0.5 * pot_ref[...]
-    call_value = ((half_pot + bet_ref[...] * pot_ref[...]) / hand_count) * margin
+    pot, bet = column(pot_ref[...]), column(bet_ref[...])
+    half_pot = 0.5 * pot
+    call_value = ((half_pot + bet * pot) / hand_count) * margin
     stake = (half_pot / hand_count) * live
     values = jnp.maximum(call_value, -stake)
     values_ref[...] = values[:, 0:own_count]
-    part = jnp.sum(values, axis=0, keepdims=True) / total_boards
-    mass = jnp.sum(stake, axis=0, keepdims=True) / total_boards
-    part = jnp.where(iota((1, lanes), 1) < own_count, part, 0.0)
-    part_ref[...] = part
-    numerator = jnp.sum(part * trav_ref[...], axis=1, keepdims=True)
-    denominator = jnp.sum(mass * trav_ref[...], axis=1, keepdims=True)
-    sums_ref[...] = jnp.where(iota((1, 128), 1) == 0, numerator, denominator)
-
-
-def compute(own, other, rank, cards, pot, bet, trav, total_boards, hand_count, own_count, me=None):
-    boards, lanes = own.shape
+    part = jnp.sum(values, axis=0, keepdims=True)[:, 0:own_count] / total_boards
+    mass = jnp.sum(stake, axis=0, keepdims=True)[:, 0:own_count] / total_boards
+    trav = trav_ref[...]
+    numerator = jnp.sum(part * trav, axis=1, keepdims=True)
+    denominator = jnp.sum(mass * trav, axis=1, keepdims=True)
+
+    spot = XS * y + x
+    mine_ref[0] = jnp.zeros((8, 128), F32)
+    for k in range(lanes // 128):
+        size = min(128, own_count - 128 * k)
+        mine_ref[0, k : k + 1, 0:size] = part[:, 128 * k : 128 * k + size]
+    mine_ref[0, 6:7, :] = jnp.where(iota((1, 128), 1) == 0, numerator, denominator)
+
+    def exchange(source, groups):
+        sent = []
+        for peers, here, slots, sems in groups:
+            for k, peer in enumerate(peers):
+                copy = pltpu.make_async_remote_copy(
+                    source, slots.at[here], sems.at[0, k], sems.at[1, here], device_id=peer, device_id_type=MESH
+                )
+                copy.start()
+                sent.append(copy)
+        return sent
+
+    def arrived(source, where, slots, sems):
+        pltpu.make_async_remote_copy(
+            source, slots.at[where], sems.at[0, 0], sems.at[1, where], device_id=plane[0], device_id_type=MESH
+        ).wait_recv()
+
+    sent = exchange(mine_ref.at[0], [(plane, spot, plane_ref, plane_sem)])
+    plane_ref[spot] = mine_ref[0]
+    for peer in plane:
+        arrived(mine_ref.at[0], XS * peer["board_0"] + peer["board_1"], plane_ref, plane_sem)
+    mine_ref[1] = functools.reduce(jnp.add, [plane_ref[k] for k in range(YS * XS)])
+    sent += exchange(mine_ref.at[1], [(line, z, line_ref, line_sem), (cross, z, cross_ref, cross_sem)])
+    line_ref[z] = mine_ref[1]
+    for peer in line:
+        arrived(mine_ref.at[1], peer["board_2"], line_ref, line_sem)
+    for peer in cross:
+        arrived(mine_ref.at[1], peer["board_2"], cross_ref, cross_sem)
+    total = functools.reduce(jnp.add, [line_ref[k] for k in range(ZS)])
+    rest = functools.reduce(jnp.add, [cross_ref[k] for k in range(ZS)])
+    hand_ref[...] = total
+    ends = total[6:7] + rest[6:7]
+    ratio_ref[...] = ends[:, 0:1] / ends[:, 1:2]
+    for copy in sent:
+        copy.wait_send()
+
+
+def local(opp_reach, hand_rank, hand_cards, pot, bet_frac, trav_reach):
+    boards, hand_count = hand_rank.shape
+    own_count = opp_reach.shape[1]
+    lanes = -(-own_count // 128) * 128
     width = 2 * lanes
+    total_boards = boards * lax.axis_size(BOARD)
     whole = pl.BlockSpec(memory_space=pltpu.VMEM)
-    return pl.pallas_call(
-        functools.partial(compute_kernel, total_boards, hand_count, own_count, me),
+    board_values, hand_rows, ratio = pl.pallas_call(
+        functools.partial(fused_kernel, total_boards, hand_count),
         out_shape=(
             jax.ShapeDtypeStruct((boards, own_count), F32),
-            jax.ShapeDtypeStruct((1, lanes), F32),
-            jax.ShapeDtypeStruct((1, 128), F32),
+            jax.ShapeDtypeStruct((8, 128), F32),
+            jax.ShapeDtypeStruct((1, 1), F32),
         ),
-        in_specs=[whole] * 7,
+        in_specs=[whole] * 6,
         out_specs=(whole,) * 3,
         scratch_shapes=[
             pltpu.VMEM((4 * boards, width), BF16),
@@ -253,40 +354,27 @@
             pltpu.VMEM((HI // 4, boards, 128), F32),
             pltpu.VMEM((boards, lanes), F32),
             pltpu.VMEM((2, width), F32),
+            pltpu.VMEM((boards, own_count), BF16),
+            pltpu.VMEM((2, 8, 128), F32),
+            pltpu.VMEM((YS * XS, 8, 128), F32),
+            pltpu.VMEM((ZS, 8, 128), F32),
+            pltpu.VMEM((ZS, 8, 128), F32),
+            pltpu.SemaphoreType.DMA((2,)),
+            pltpu.SemaphoreType.DMA((2, YS * XS)),
+            pltpu.SemaphoreType.DMA((2, ZS)),
+            pltpu.SemaphoreType.DMA((2, ZS)),
         ],
-        compiler_params=pltpu.CompilerParams(vmem_limit_bytes=56 * 1024 * 1024),
+        compiler_params=pltpu.CompilerParams(
+            vmem_limit_bytes=56 * 1024 * 1024, collective_id=0, has_side_effects=True
+        ),
         cost_estimate=pl.CostEstimate(flops=10**9, bytes_accessed=10**6, transcendentals=0),
-    )(own, other, rank, cards, pot, bet, trav)
-
-
-def local(opp_reach, hand_rank, hand_cards, pot, bet_frac, trav_reach):
-    boards, hand_count = hand_rank.shape
-    own_count = opp_reach.shape[1]
-    lanes = -(-own_count // 128) * 128
-    gap = lanes - own_count
-    total_boards = boards * lax.axis_size(BOARD)
-    own = jnp.pad(opp_reach, ((0, 0), (0, gap)))
-    other = lax.ppermute(own, "hand", [(0, 1), (1, 0)])
-    rank = jnp.pad(hand_rank.reshape(boards, 2, own_count).transpose(1, 0, 2), ((0, 0), (0, 0), (0, gap)))
-    cards = jnp.pad(
-        hand_cards.reshape(2, own_count, 2).transpose(0, 2, 1).astype(F32),
-        ((0, 0), (0, 0), (0, gap)),
-        constant_values=-1.0,
-    )
-    trav = jnp.pad(trav_reach, (0, gap))[None, :]
-    board_values, part, sums = compute(
-        own, other, rank, cards, pot[:, None], bet_frac[:, None], trav, total_boards, hand_count, own_count
-    )
-    packed = jnp.concatenate([part, sums], axis=1)
-    packed = functools.reduce(lax.psum, BOARD, packed)
-    hand_values = packed[0, :own_count]
-    ends = lax.psum(packed[0, lanes : lanes + 2], "hand")
-    return board_values, hand_values, ends[0] / ends[1]
+    )(opp_reach, hand_rank, hand_cards.T, pot[None, :], bet_frac[None, :], trav_reach[None, :])
+    return board_values, hand_rows.reshape(-1)[:own_count], ratio[0, 0]
 
 
 def solution(mesh):
     torus = Mesh(
-        mesh.devices.reshape(4, 4, 8, mesh.shape["hand"]), ("board_0", "board_1", "board_2", "hand")
+        mesh.devices.reshape(YS, XS, ZS, mesh.shape["hand"]), ("board_0", "board_1", "board_2", "hand")
     )
     placed = (P(BOARD, "hand"), P(BOARD, None), P(), P(BOARD), P(BOARD), P("hand"))
     return jax.shard_map(

time: 83.1 us -> 50.2 us (0.60)
  blocking collectives: 41.6 us -> 0 us
  Pallas kernels: 24.3 us -> 44.2 us
  local copies, waits for them, and re-layouts: 10.2 us -> 3.47 us
  starting transfers between devices: 3.29 us -> 0 us
    psum x4 -> x0, blocking collectives: 41.6 us -> none  [the longest x3 31.9 us: local(): packed = functools.reduce(lax.psum, BOARD, packed)]
    pallas_call x1, Pallas kernels: 24.3 us -> 44.2 us  [local(): pl.pallas_call(functools.partial(fused_kernel, total_boards, hand_count),...]
    ppermute x1 -> x0, starting transfers between devices: 3.29 us -> none  [local(): other = lax.ppermute(own, 'hand', [(0, 1), (1, 0)])]
    pad x4 -> x0, local copies, waits for them, and re-layouts: 2.27 us -> none  [the longest x1 0.91 us: local(): own = jnp.pad(opp_reach, ((0, 0), (0, gap)))]
    broadcast_in_dim x3 -> x1, local copies, waits for them, and re-layouts: 1.98 us -> 0.58 us  [local(): trav_reach[None, :]]
    reshape x2 -> x0, local copies, waits for them, and re-layouts: 1.38 us -> none  [local(): hand_rank.reshape(boards, 2, own_count).transpose(1, 0, 2)]
    slice x2 -> x0, local copies, waits for them, and re-layouts: 1.2 us -> none  [the longest x1 0.61 us: local(): hand_values = packed[0, :own_count]]
    unnamed x16 -> x6, local copies, waits for them, and re-layouts: 3.29 us -> 2.89 us
  transfers between devices with their start and end apart: 1 -> 0, of which waited for: 0 -> 0; matrix products, arithmetic and copies ran while one was open for 6% -> 0% of each run, Pallas kernels for 0% -> 0%
where the time goes in v2:
time: 50.2 us; the launch traced here: 50.1 us
  Pallas kernels  44.2 us (88%)
  local copies, waits for them, and re-layouts  3.47 us (7%)
  between operations  2.41 us (5%)
    pallas_call x1, Pallas kernels, local(): pl.pallas_call(functools.partial(fused_kernel, total_boards, hand_count),...  44.2 us
    unnamed x6, local copies, waits for them, and re-layouts  2.89 us

profile of v2, /device:TPU:1, one launch (start us, length us, event | category | flops | bytes accessed | tf_op | source)
XLA Modules:
  0.0 50.1 jit_solution(7957832330145350379)
XLA Ops:
  0.6 0.0 copy-start
  0.6 0.7 %copy-done = f32[663]{0:T(1024)S(1)} copy-done((f32[663]{0:T(1024)S(1)}, f32[663]{0:T(1024)}, u32[]{:S(2)}) %copy-start) | copy-done | bytes 2676
  1.3 0.6 %broadcast_in_dim.11.trav_ref = f32[1,663]{1,0:T(1,128)} reshape(f32[663]{0:T(1024)S(1)} %copy-done) | data formatting | bytes 5304 | tf_op jit(solution)/shard_map/broadcast_in_dim | solution.py:371
  1.9 44.2 %shard_map.85 = (f32[64,663]{1,0:T(8,128)}, f32[8,128]{1,0:T(8,128)}, f32[1,1]{1,0:T(1,128)}) custom-call(bf16[64,663]{1,0:T(8,128)(2,1)} %reach_ref.1, s32[64,1326]{1,0:T(8,128)} %rank_ref.1, s32[2,1326]{1,0:T(2,128)} %bitcast.7, f32[1,64]{1,0:T(1,128)} %bitcast.8, f32[1,64]{1,0:T(1,128)} %bitcast.9, f32[1,663]{1,0:T(1,128)} %broadcast_in_dim.11.trav_ref), custom_call_target="tpu_custom_call" | custom-call | flops 1000000000 | bytes 1000000 | tf_op jit(solution)/shard_map/pallas_call | solution.py:334
  46.1 0.0 copy-start.1
  46.1 1.6 %copy.12 = f32[64,663]{1,0:T(8,128)} copy(f32[64,663]{1,0:T(8,128)} %get-tuple-element.12) | data formatting | bytes 339456
  47.7 0.0 copy-done.1
  47.7 0.6 %copy.13 = f32[663]{0:T(1024)} copy(f32[663]{0:T(1024)S(1)} %bitcast.6) | data formatting | bytes 5304
Async XLA Ops:
  0.6 0.7 %copy-start = (f32[663]{0:T(1024)S(1)}, f32[663]{0:T(1024)}, u32[]{:S(2)}) copy-start(f32[663]{0:T(1024)} %param.11) | copy-start | bytes 7960
  46.1 1.6 %copy-start.1 = (f32[8,128]{1,0:T(8,128)S(1)}, f32[8,128]{1,0:T(8,128)}, u32[]{:S(2)}) copy-start(f32[8,128]{1,0:T(8,128)} %get-tuple-element.7) | copy-start | bytes 12292

commit v3 on v2

v3 whole, which is shorter than its diff:
```python
import functools

import jax
import jax.numpy as jnp
from jax import lax
from jax.experimental import pallas as pl
from jax.experimental.pallas import tpu as pltpu
from jax.sharding import Mesh
from jax.sharding import PartitionSpec as P

CARDS = 52
BOARD = ("board_0", "board_1", "board_2")
BF16 = jnp.bfloat16
F32 = jnp.float32

PARTS = 4
SHARE = CARDS // PARTS
ROWS = 16
HI, LO = 48, 28
SLOT = 32
GROUP = 8
DBLOCK = 4
YS, XS, ZS = 4, 4, 8
MESH = pl.DeviceIdType.MESH
NT = (((1,), (1,)), ((), ()))


def iota(shape, axis):
    return lax.broadcasted_iota(jnp.int32, shape, axis)


def split2(x):
    high = x.astype(BF16)
    return high, (x - high.astype(F32)).astype(BF16)


def rank_code(rank):
    return (((rank & 127) | 128) << (rank >> 7)).astype(F32).astype(BF16)


def every_peer(places):
    y, x, z, h = places
    plane = [
        {"board_0": lax.rem(y + i, YS), "board_1": lax.rem(x + j, XS)}
        for i in range(YS)
        for j in range(XS)
        if i or j
    ]
    line = [{"board_2": lax.rem(z + i, ZS)} for i in range(1, ZS)]
    cross = [{"board_2": lax.rem(z + i, ZS), "hand": 1 - h} for i in range(ZS)]
    return plane, line, cross


def column(row, start, size):
    n = row.shape[1]
    hit = iota((size, n), 1) == iota((size, n), 0) + start
    return jnp.sum(jnp.where(hit, row, 0.0), axis=1, keepdims=True)


def fused_kernel(
    total_boards, hand_count,
    reach_ref, rank_ref, cards_ref, pot_ref, bet_ref, trav_ref,
    values_ref, hand_ref, ratio_ref,
    x_ref, p_ref, o_ref, w_ref, g_ref, q_ref, f_ref, a_ref, b_ref, h_ref, t_ref, s_ref, c_ref, k_ref,
    swap_ref, mine_ref, plane_ref, line_ref, cross_ref,
    swap_sem, pair_sem, total_sem, sum_sem, plane_sem, line_sem, cross_sem,
):
    all_boards, own_count = reach_ref.shape
    boards = all_boards // 2
    block = 4 * boards
    lanes = x_ref.shape[1] // 2
    width = 2 * lanes
    places = tuple(lax.axis_index(name) for name in BOARD) + (lax.axis_index("hand"),)
    y, x, z, me = places
    plane, line, cross = every_peer(places)
    barrier = pltpu.get_barrier_semaphore()
    for peer in plane + line + cross:
        pl.semaphore_signal(barrier, inc=1, device_id=peer, device_id_type=MESH)

    def cols_of(half, start=0, size=lanes):
        return pl.ds(pl.multiple_of(half * lanes + start, 128), size)

    def rows_of(core):
        return pl.ds(pl.multiple_of(core * boards, boards), boards)

    def to_partner(source, target, sems):
        copy = pltpu.make_async_remote_copy(
            source, target, sems.at[0], sems.at[1], device_id={"hand": 1 - me}, device_id_type=MESH
        )
        copy.start()
        return copy

    for half in range(2):
        start = half * lanes
        c_ref[:, start + lanes - 128 : start + lanes] = jnp.full((2, 128), -1.0, F32)
        c_ref[:, start : start + own_count] = cards_ref[:, half * own_count : (half + 1) * own_count].astype(F32)

    row16 = iota((16, width), 0)
    own_row = [
        jnp.where(row16 < SHARE, row16 + SHARE * q, -5).astype(F32).astype(BF16) for q in range(PARTS)
    ]

    def hot_rows(d, carry):
        low, high = c_ref[0:1, :], c_ref[1:2, :]
        df = d.astype(F32)
        partner = jnp.where(low == df, high, jnp.where(high == df, low, -1.0))
        wide = jnp.broadcast_to(partner, (16, width)).astype(BF16)
        for q in range(PARTS):
            p_ref[q, d] = jnp.where(wide == own_row[q], BF16(1), BF16(0))
        return carry

    lax.fori_loop(0, CARDS, hot_rows, 0)

    for half in range(2):
        start = half * lanes
        f_ref[0:2, :, start + lanes - 128 : start + lanes] = jnp.zeros((2, boards, 128), F32)
        x_ref[:, start + lanes - 128 : start + lanes] = jnp.zeros((8 * boards, 128), BF16)
        rank = rank_ref[rows_of(me), half * own_count : (half + 1) * own_count]
        x_ref[block : block + boards, start : start + own_count] = rank_code(rank)
        hi = (rank * 2341) >> 16
        f_ref[0, :, start : start + own_count] = hi.astype(F32)
        f_ref[1, :, start : start + own_count] = (rank - LO * hi).astype(F32)
    for k in range(1, PARTS):
        x_ref[block + k * boards : block + (k + 1) * boards, :] = x_ref[block : block + boards, :]

    def place(half, reach):
        x_ref[0:boards, pl.ds(pl.multiple_of(half * lanes, 128), own_count)] = reach
        for k in range(1, PARTS):
            x_ref[k * boards : (k + 1) * boards, cols_of(half)] = x_ref[0:boards, cols_of(half)]

    def to_cards(half, more):
        def one(q, carry):
            rows = p_ref[q, :, :, cols_of(half)].reshape(CARDS * ROWS, lanes)
            got = lax.dot_general(rows, x_ref[:, cols_of(half)], NT, preferred_element_type=F32)
            got = got.reshape(CARDS, ROWS, 2 * block)
            if more:
                got = got + o_ref[q]
            o_ref[q] = got
            return carry

        lax.fori_loop(0, PARTS, one, 0)

    place(me, reach_ref[rows_of(me), :])
    pl.semaphore_wait(barrier, len(plane + line + cross))
    swap = to_partner(reach_ref.at[rows_of(1 - me), :], swap_ref, swap_sem)
    to_cards(me, False)
    swap.wait()
    place(1 - me, swap_ref[...])
    to_cards(1 - me, True)
    f_ref[2] = x_ref[0:boards, :].astype(F32)

    part_of = iota((ROWS, block), 1) // boards

    def pack(d, carry):
        for ref, at in ((w_ref, 0), (g_ref, block)):
            got = o_ref[0, d, :, at : at + block]
            for q in range(1, PARTS):
                got = jnp.where(part_of == q, o_ref[q, d, :, at : at + block], got)
            ref[d] = got
        return carry

    lax.fori_loop(0, CARDS, pack, 0)

    def pairs(i, carry):
        mine = [g_ref[DBLOCK * i + k].astype(BF16) for k in range(DBLOCK)]
        sums = [None] * DBLOCK
        for e in range(CARDS):
            ge, we = g_ref[e].astype(BF16), w_ref[e].astype(BF16)
            for k in range(DBLOCK):
                sign = lax.clamp(BF16(-1), mine[k] - ge, BF16(1))
                term = sign.astype(F32) * we.astype(F32)
                sums[k] = term if sums[k] is None else sums[k] + term
        for k in range(DBLOCK):
            q_ref[0, DBLOCK * i + k] = sums[k]
        return carry

    lax.fori_loop(0, CARDS // DBLOCK, pairs, 0)
    pair_copy = to_partner(q_ref.at[0], q_ref.at[1], pair_sem)

    card = iota((64, lanes), 0).astype(F32)
    card_totals = jnp.zeros((boards, 64), F32)
    for half in (1 - me, me):
        hold = ((card == c_ref[0:1, cols_of(half)]) | (card == c_ref[1:2, cols_of(half)])).astype(F32).astype(BF16)
        card_totals = card_totals + lax.dot_general(
            x_ref[0:boards, cols_of(half)], hold, NT, preferred_element_type=F32
        )
    k_ref[0] = jnp.concatenate([card_totals, jnp.zeros((boards, 64), F32)], axis=1)
    total_copy = to_partner(k_ref.at[0], k_ref.at[1], total_sem)

    lo_row = row16.astype(F32).astype(BF16)
    even = iota((GROUP, 128), 0) % 2 == 0
    slot = ((iota((GROUP, 128), 1) + SLOT // 2 * iota((GROUP, 128), 0)) % 128) // SLOT
    tiles = HI // 4
    for g in range(boards // GROUP):
        now = g % 2
        for b in range(GROUP):
            at = GROUP * g + b
            hi = jnp.broadcast_to(f_ref[0, at : at + 1, :], (16, width)).astype(BF16)
            lo = jnp.broadcast_to(f_ref[1, at : at + 1, :], (16, width)).astype(BF16)
            reach = jnp.broadcast_to(f_ref[2, at : at + 1, :], (16, width)).astype(BF16)
            tile, start = 128 * (b % 2), 128 - SLOT // 2 * b
            for part in range(HI // 16):
                hit = hi == lo_row + BF16(16 * part)
                a_ref[now, HI * b + 16 * part : HI * b + 16 * part + 16, :] = jnp.where(hit, reach, BF16(0))
            for part in range(SLOT // 16):
                at = tile + (start + 16 * part) % 128
                b_ref[now, at : at + 16, :] = lax.clamp(BF16(-1), lo_row + BF16(16 * part) - lo, BF16(1))
        got = lax.dot_general(a_ref[now], b_ref[now], NT, preferred_element_type=F32)
        h_ref[now, 0 : GROUP * HI, :] = got[:, 0:128]
        h_ref[now, GROUP * HI :, :] = got[:, 128:256]
        for t in range(tiles):
            row = None
            for k in range(4):
                at = 4 * t + k
                part = jnp.where(
                    even,
                    h_ref[now, pl.ds(at, GROUP, stride=HI), :],
                    h_ref[now, pl.ds(at + GROUP * HI, GROUP, stride=HI), :],
                )
                part = pltpu.roll(part, SLOT * k, 1) if k else part
                row = part if row is None else jnp.where(slot == k, part, row)
            t_ref[t, GROUP * g : GROUP * (g + 1), :] = pltpu.roll(row, 0, 1, stride=SLOT // 2, stride_axis=0)

    spot = iota((boards, 128), 1) % SLOT == LO
    below = []
    run = jnp.zeros((boards, 128), F32)
    whole = []
    for t in range(tiles):
        mark = jnp.where(spot, t_ref[t], 0.0)
        whole.append(mark)
        below.append(run)
        run = run + mark
    src, dst = iota((256, 128), 0), iota((256, 128), 1)
    within = (dst // SLOT > (src - 128) // SLOT).astype(F32) - (dst // SLOT < (src - 128) // SLOT).astype(F32)
    spread = jnp.where(src % SLOT == LO, jnp.where(src < 128, 1.0, within), 0.0).astype(BF16)
    both = jnp.concatenate(
        [jnp.concatenate([below[t] - (run - below[t] - whole[t]), whole[t]], axis=1) for t in range(tiles)], axis=0
    )
    high, low = split2(both)
    got = jnp.dot(high, spread, preferred_element_type=F32) + jnp.dot(low, spread, preferred_element_type=F32)
    for t in range(tiles):
        t_ref[t] = t_ref[t] + got[boards * t : boards * (t + 1)]

    for half in (1 - me, me):

        def look_up(g, carry):
            rows = pl.ds(pl.multiple_of(GROUP * g, GROUP), GROUP)
            for k in range(lanes // 128):
                hi = f_ref[0, rows, cols_of(half, 128 * k, 128)].astype(jnp.int32)
                lo = f_ref[1, rows, cols_of(half, 128 * k, 128)].astype(jnp.int32)
                tile = hi >> 2
                at = ((hi & 3) << 5) + lo
                found = jnp.zeros((GROUP, 128), F32)
                for t in range(tiles):
                    got = jnp.take_along_axis(t_ref[t, rows, :], at, axis=1, mode="promise_in_bounds")
                    found = jnp.where(tile == t, got, found)
                s_ref[half, rows, 128 * k : 128 * k + 128] = found
            return carry

        lax.fori_loop(0, boards // GROUP, look_up, 0)
        if half is not me:
            sum_copy = to_partner(s_ref.at[1 - me], s_ref.at[2], sum_sem)

    pair_copy.wait()
    total_copy.wait()
    turned = [jnp.transpose(q_ref[k].reshape(CARDS * ROWS, block)) for k in range(2)]
    shared = jnp.zeros((4 * boards, lanes), F32)
    for q in range(PARTS):
        pieces = [split2(t[boards * q : boards * (q + 1)]) for t in turned]
        shared = shared + jnp.dot(
            jnp.concatenate([piece for pair in pieces for piece in pair], axis=0),
            p_ref[q, :, :, cols_of(me)].reshape(CARDS * ROWS, lanes),
            preferred_element_type=F32,
        )
    pieces = [split2(k_ref[k][:, 0:64]) for k in range(2)]
    held = jnp.dot(
        jnp.concatenate([piece for pair in pieces for piece in pair], axis=0), hold, preferred_element_type=F32
    )
    sum_copy.wait()
    part = mass = None
    for k, core in ((0, me), (1, 1 - me)):
        at = 2 * boards * k
        live = (
            0.5 * jnp.sum(k_ref[k][:, 0:64], axis=1, keepdims=True)
            - (held[at : at + boards] + held[at + boards : at + 2 * boards])
        )[:, 0:own_count] + reach_ref[rows_of(core), :].astype(F32)
        sums = s_ref[me] if k == 0 else s_ref[2]
        margin = (sums - (shared[at : at + boards] + shared[at + boards : at + 2 * boards]))[:, 0:own_count]
        pot = column(pot_ref[...], core * boards, boards)
        bet = column(bet_ref[...], core * boards, boards)
        half_pot = 0.5 * pot
        stake = (half_pot / hand_count) * live
        values = jnp.maximum(((half_pot + bet * pot) / hand_count) * margin, -stake)
        values_ref[rows_of(core), :] = values
        values, stake = (jnp.sum(v, axis=0, keepdims=True) for v in (values, stake))
        part = values if part is None else part + values
        mass = stake if mass is None else mass + stake
    part, mass = part / total_boards, mass / total_boards
    trav = trav_ref[...]
    numerator = jnp.sum(part * trav, axis=1, keepdims=True)
    denominator = jnp.sum(mass * trav, axis=1, keepdims=True)

    spot = XS * y + x
    mine_ref[0] = jnp.zeros((8, 128), F32)
    for k in range(lanes // 128):
        size = min(128, own_count - 128 * k)
        mine_ref[0, k : k + 1, 0:size] = part[:, 128 * k : 128 * k + size]
    mine_ref[0, 6:7, :] = jnp.where(iota((1, 128), 1) == 0, numerator, denominator)

    def exchange(source, groups):
        sent = []
        for peers, here, slots, sems in groups:
            for k, peer in enumerate(peers):
                copy = pltpu.make_async_remote_copy(
                    source, slots.at[here], sems.at[0, k], sems.at[1, here], device_id=peer, device_id_type=MESH
                )
                copy.start()
                sent.append(copy)
        return sent

    def arrived(source, where, slots, sems):
        pltpu.make_async_remote_copy(
            source, slots.at[where], sems.at[0, 0], sems.at[1, where], device_id=plane[0], device_id_type=MESH
        ).wait_recv()

    sent = exchange(mine_ref.at[0], [(plane, spot, plane_ref, plane_sem)])
    plane_ref[spot] = mine_ref[0]
    for peer in plane:
        arrived(mine_ref.at[0], XS * peer["board_0"] + peer["board_1"], plane_ref, plane_sem)
    mine_ref[1] = functools.reduce(jnp.add, [plane_ref[k] for k in range(YS * XS)])
    sent += exchange(mine_ref.at[1], [(line, z, line_ref, line_sem), (cross, z, cross_ref, cross_sem)])
    line_ref[z] = mine_ref[1]
    for peer in line:
        arrived(mine_ref.at[1], peer["board_2"], line_ref, line_sem)
    for peer in cross:
        arrived(mine_ref.at[1], peer["board_2"], cross_ref, cross_sem)
    total = functools.reduce(jnp.add, [line_ref[k] for k in range(ZS)])
    rest = functools.reduce(jnp.add, [cross_ref[k] for k in range(ZS)])
    hand_ref[...] = total
    ends = total[6:7] + rest[6:7]
    ratio_ref[...] = ends[:, 0:1] / ends[:, 1:2]
    for copy in sent:
        copy.wait_send()


def local(opp_reach, hand_rank, hand_cards, pot, bet_frac, trav_reach):
    boards, hand_count = hand_rank.shape
    own_count = opp_reach.shape[1]
    lanes = -(-own_count // 128) * 128
    width = 2 * lanes
    half = boards // 2
    total_boards = boards * lax.axis_size(BOARD)
    whole = pl.BlockSpec(memory_space=pltpu.VMEM)
    board_values, hand_rows, ratio = pl.pallas_call(
        functools.partial(fused_kernel, total_boards, hand_count),
        out_shape=(
            jax.ShapeDtypeStruct((boards, own_count), F32),
            jax.ShapeDtypeStruct((8, 128), F32),
            jax.ShapeDtypeStruct((1, 1), F32),
        ),
        in_specs=[whole] * 6,
        out_specs=(whole,) * 3,
        scratch_shapes=[
            pltpu.VMEM((8 * half, width), BF16),
            pltpu.VMEM((PARTS, CARDS, ROWS, width), BF16),
            pltpu.VMEM((PARTS, CARDS, ROWS, 8 * half), F32),
            pltpu.VMEM((CARDS, ROWS, 4 * half), F32),
            pltpu.VMEM((CARDS, ROWS, 4 * half), F32),
            pltpu.VMEM((2, CARDS, ROWS, 4 * half), F32),
            pltpu.VMEM((3, half, width), F32),
            pltpu.VMEM((2, GROUP * HI, width), BF16),
            pltpu.VMEM((2, GROUP * SLOT, width), BF16),
            pltpu.VMEM((2, 2 * GROUP * HI, 128), F32),
            pltpu.VMEM((HI // 4, half, 128), F32),
            pltpu.VMEM((3, half, lanes), F32),
            pltpu.VMEM((2, width), F32),
            pltpu.VMEM((2, half, 128), F32),
            pltpu.VMEM((half, own_count), BF16),
            pltpu.VMEM((2, 8, 128), F32),
            pltpu.VMEM((YS * XS, 8, 128), F32),
            pltpu.VMEM((ZS, 8, 128), F32),
            pltpu.VMEM((ZS, 8, 128), F32),
            pltpu.SemaphoreType.DMA((2,)),
            pltpu.SemaphoreType.DMA((2,)),
            pltpu.SemaphoreType.DMA((2,)),
            pltpu.SemaphoreType.DMA((2,)),
            pltpu.SemaphoreType.DMA((2, YS * XS)),
            pltpu.SemaphoreType.DMA((2, ZS)),
            pltpu.SemaphoreType.DMA((2, ZS)),
        ],
        compiler_params=pltpu.CompilerParams(
            vmem_limit_bytes=56 * 1024 * 1024, collective_id=0, has_side_effects=True
        ),
        cost_estimate=pl.CostEstimate(flops=10**9, bytes_accessed=10**6, transcendentals=0),
    )(opp_reach, hand_rank, hand_cards.T, pot[None, :], bet_frac[None, :], trav_reach[None, :])
    return board_values, hand_rows.reshape(-1)[:own_count], ratio[0, 0]


def solution(mesh):
    torus = Mesh(
        mesh.devices.reshape(YS, XS, ZS, mesh.shape["hand"]), ("board_0", "board_1", "board_2", "hand")
    )
    placed = (P(BOARD, "hand"), P(BOARD, None), P(), P(BOARD), P(BOARD), P("hand"))
    return jax.shard_map(
        local,
        mesh=torus,
        in_specs=placed,
        out_specs=(P(BOARD, "hand"), P("hand"), P()),
        check_vma=False,
    )
```

time: 50.2 us -> 39.7 us (0.79)
  Pallas kernels: 44.2 us -> 33.6 us
    pallas_call x1, Pallas kernels: 44.2 us -> 33.6 us  [local(): pl.pallas_call(functools.partial(fused_kernel, total_boards, hand_count),...]
where the time goes in v3:
time: 39.7 us; the launch traced here: 39.5 us
  Pallas kernels  33.6 us (85%)
  local copies, waits for them, and re-layouts  3.47 us (9%)
  between operations  2.41 us (6%)
    pallas_call x1, Pallas kernels, local(): pl.pallas_call(functools.partial(fused_kernel, total_boards, hand_count),...  33.6 us
    unnamed x6, local copies, waits for them, and re-layouts  2.89 us

profile of v3, /device:TPU:1, one launch (start us, length us, event | category | flops | bytes accessed | tf_op | source)
XLA Modules:
  0.0 39.5 jit_solution(3714611729834927787)
XLA Ops:
  0.6 0.0 copy-start
  0.6 0.7 %copy-done = f32[663]{0:T(1024)S(1)} copy-done((f32[663]{0:T(1024)S(1)}, f32[663]{0:T(1024)}, u32[]{:S(2)}) %copy-start) | copy-done | bytes 2676
  1.3 0.6 %broadcast_in_dim.11.trav_ref = f32[1,663]{1,0:T(1,128)} reshape(f32[663]{0:T(1024)S(1)} %copy-done) | data formatting | bytes 5304 | tf_op jit(solution)/shard_map/broadcast_in_dim | solution.py:395
  1.9 33.6 %shard_map.85 = (f32[64,663]{1,0:T(8,128)}, f32[8,128]{1,0:T(8,128)}, f32[1,1]{1,0:T(1,128)}) custom-call(bf16[64,663]{1,0:T(8,128)(2,1)} %reach_ref.1, s32[64,1326]{1,0:T(8,128)} %rank_ref.1, s32[2,1326]{1,0:T(2,128)} %bitcast.7, f32[1,64]{1,0:T(1,128)} %bitcast.8, f32[1,64]{1,0:T(1,128)} %bitcast.9, f32[1,663]{1,0:T(1,128)} %broadcast_in_dim.11.trav_ref), custom_call_target="tpu_custom_call" | custom-call | flops 1000000000 | bytes 1000000 | tf_op jit(solution)/shard_map/pallas_call | solution.py:354
  35.6 0.0 copy-start.1
  35.6 1.6 %copy.12 = f32[64,663]{1,0:T(8,128)} copy(f32[64,663]{1,0:T(8,128)} %get-tuple-element.12) | data formatting | bytes 339456
  37.2 0.0 copy-done.1
  37.2 0.6 %copy.13 = f32[663]{0:T(1024)} copy(f32[663]{0:T(1024)S(1)} %bitcast.6) | data formatting | bytes 5304
Async XLA Ops:
  0.6 0.7 %copy-start = (f32[663]{0:T(1024)S(1)}, f32[663]{0:T(1024)}, u32[]{:S(2)}) copy-start(f32[663]{0:T(1024)} %param.11) | copy-start | bytes 7960
  35.6 1.6 %copy-start.1 = (f32[8,128]{1,0:T(8,128)S(1)}, f32[8,128]{1,0:T(8,128)}, u32[]{:S(2)}) copy-start(f32[8,128]{1,0:T(8,128)} %get-tuple-element.7) | copy-start | bytes 12292

commit v4 on v3

--- a/solution.py
+++ b/solution.py
@@ -59,8 +59,9 @@
 
 def fused_kernel(
     total_boards, hand_count,
-    reach_ref, rank_ref, cards_ref, pot_ref, bet_ref, trav_ref,
-    values_ref, hand_ref, ratio_ref,
+    reach_hbm, rank_hbm, cards_hbm, pot_hbm, bet_hbm, trav_hbm,
+    values_hbm, hand_ref, ratio_ref,
+    reach_ref, rank_ref, cards_ref, pot_ref, bet_ref, trav_ref, values_ref, io_sem,
     x_ref, p_ref, o_ref, w_ref, g_ref, q_ref, f_ref, a_ref, b_ref, h_ref, t_ref, s_ref, c_ref, k_ref,
     swap_ref, mine_ref, plane_ref, line_ref, cross_ref,
     swap_sem, pair_sem, total_sem, sum_sem, plane_sem, line_sem, cross_sem,
@@ -74,8 +75,6 @@
     y, x, z, me = places
     plane, line, cross = every_peer(places)
     barrier = pltpu.get_barrier_semaphore()
-    for peer in plane + line + cross:
-        pl.semaphore_signal(barrier, inc=1, device_id=peer, device_id_type=MESH)
 
     def cols_of(half, start=0, size=lanes):
         return pl.ds(pl.multiple_of(half * lanes + start, 128), size)
@@ -90,6 +89,25 @@
         copy.start()
         return copy
 
+    loads = [
+        pltpu.make_async_copy(source, target, io_sem.at[k])
+        for k, (source, target) in enumerate(
+            (
+                (cards_hbm, cards_ref),
+                (rank_hbm.at[rows_of(me), :], rank_ref),
+                (reach_hbm, reach_ref),
+                (pot_hbm, pot_ref),
+                (bet_hbm, bet_ref),
+                (trav_hbm, trav_ref),
+            )
+        )
+    ]
+    for load in loads:
+        load.start()
+    for peer in plane + line + cross:
+        pl.semaphore_signal(barrier, inc=1, device_id=peer, device_id_type=MESH)
+
+    loads[0].wait()
     for half in range(2):
         start = half * lanes
         c_ref[:, start + lanes - 128 : start + lanes] = jnp.full((2, 128), -1.0, F32)
@@ -111,11 +129,13 @@
 
     lax.fori_loop(0, CARDS, hot_rows, 0)
 
+    loads[1].wait()
+    loads[2].wait()
     for half in range(2):
         start = half * lanes
         f_ref[0:2, :, start + lanes - 128 : start + lanes] = jnp.zeros((2, boards, 128), F32)
         x_ref[:, start + lanes - 128 : start + lanes] = jnp.zeros((8 * boards, 128), BF16)
-        rank = rank_ref[rows_of(me), half * own_count : (half + 1) * own_count]
+        rank = rank_ref[:, half * own_count : (half + 1) * own_count]
         x_ref[block : block + boards, start : start + own_count] = rank_code(rank)
         hi = (rank * 2341) >> 16
         f_ref[0, :, start : start + own_count] = hi.astype(F32)
@@ -125,29 +145,48 @@
 
     def place(half, reach):
         x_ref[0:boards, pl.ds(pl.multiple_of(half * lanes, 128), own_count)] = reach
+        f_ref[2, :, cols_of(half)] = x_ref[0:boards, cols_of(half)].astype(F32)
         for k in range(1, PARTS):
             x_ref[k * boards : (k + 1) * boards, cols_of(half)] = x_ref[0:boards, cols_of(half)]
 
     def to_cards(half, more):
-        def one(q, carry):
+        for q in range(PARTS):
             rows = p_ref[q, :, :, cols_of(half)].reshape(CARDS * ROWS, lanes)
             got = lax.dot_general(rows, x_ref[:, cols_of(half)], NT, preferred_element_type=F32)
             got = got.reshape(CARDS, ROWS, 2 * block)
-            if more:
-                got = got + o_ref[q]
-            o_ref[q] = got
-            return carry
-
-        lax.fori_loop(0, PARTS, one, 0)
+            o_ref[q] = got + o_ref[q] if more else got
+
+    digit = iota((16, lanes), 0).astype(F32).astype(BF16)
+
+    def high_factor(half):
+        for b in range(boards):
+            hi = jnp.broadcast_to(f_ref[0, b : b + 1, cols_of(half)], (16, lanes)).astype(BF16)
+            reach = jnp.broadcast_to(f_ref[2, b : b + 1, cols_of(half)], (16, lanes)).astype(BF16)
+            for part in range(HI // 16):
+                at = HI * (b % GROUP) + 16 * part
+                hit = hi == digit + BF16(16 * part)
+                a_ref[b // GROUP, at : at + 16, cols_of(half)] = jnp.where(hit, reach, BF16(0))
+
+    def low_factor(half):
+        for b in range(boards):
+            lo = jnp.broadcast_to(f_ref[1, b : b + 1, cols_of(half)], (16, lanes)).astype(BF16)
+            for part in range(SLOT // 16):
+                at = 128 * (b % 2) + (128 - SLOT // 2 * (b % GROUP) + 16 * part) % 128
+                b_ref[b // GROUP, at : at + 16, cols_of(half)] = lax.clamp(
+                    BF16(-1), digit + BF16(16 * part) - lo, BF16(1)
+                )
 
     place(me, reach_ref[rows_of(me), :])
+    to_cards(me, False)
     pl.semaphore_wait(barrier, len(plane + line + cross))
     swap = to_partner(reach_ref.at[rows_of(1 - me), :], swap_ref, swap_sem)
-    to_cards(me, False)
+    low_factor(0)
+    low_factor(1)
+    high_factor(me)
     swap.wait()
     place(1 - me, swap_ref[...])
+    high_factor(1 - me)
     to_cards(1 - me, True)
-    f_ref[2] = x_ref[0:boards, :].astype(F32)
 
     part_of = iota((ROWS, block), 1) // boards
 
@@ -187,25 +226,12 @@
     k_ref[0] = jnp.concatenate([card_totals, jnp.zeros((boards, 64), F32)], axis=1)
     total_copy = to_partner(k_ref.at[0], k_ref.at[1], total_sem)
 
-    lo_row = row16.astype(F32).astype(BF16)
     even = iota((GROUP, 128), 0) % 2 == 0
     slot = ((iota((GROUP, 128), 1) + SLOT // 2 * iota((GROUP, 128), 0)) % 128) // SLOT
     tiles = HI // 4
     for g in range(boards // GROUP):
         now = g % 2
-        for b in range(GROUP):
-            at = GROUP * g + b
-            hi = jnp.broadcast_to(f_ref[0, at : at + 1, :], (16, width)).astype(BF16)
-            lo = jnp.broadcast_to(f_ref[1, at : at + 1, :], (16, width)).astype(BF16)
-            reach = jnp.broadcast_to(f_ref[2, at : at + 1, :], (16, width)).astype(BF16)
-            tile, start = 128 * (b % 2), 128 - SLOT // 2 * b
-            for part in range(HI // 16):
-                hit = hi == lo_row + BF16(16 * part)
-                a_ref[now, HI * b + 16 * part : HI * b + 16 * part + 16, :] = jnp.where(hit, reach, BF16(0))
-            for part in range(SLOT // 16):
-                at = tile + (start + 16 * part) % 128
-                b_ref[now, at : at + 16, :] = lax.clamp(BF16(-1), lo_row + BF16(16 * part) - lo, BF16(1))
-        got = lax.dot_general(a_ref[now], b_ref[now], NT, preferred_element_type=F32)
+        got = lax.dot_general(a_ref[g], b_ref[g], NT, preferred_element_type=F32)
         h_ref[now, 0 : GROUP * HI, :] = got[:, 0:128]
         h_ref[now, GROUP * HI :, :] = got[:, 128:256]
         for t in range(tiles):
@@ -242,9 +268,8 @@
         t_ref[t] = t_ref[t] + got[boards * t : boards * (t + 1)]
 
     for half in (1 - me, me):
-
-        def look_up(g, carry):
-            rows = pl.ds(pl.multiple_of(GROUP * g, GROUP), GROUP)
+        for g in range(boards // GROUP):
+            rows = slice(GROUP * g, GROUP * (g + 1))
             for k in range(lanes // 128):
                 hi = f_ref[0, rows, cols_of(half, 128 * k, 128)].astype(jnp.int32)
                 lo = f_ref[1, rows, cols_of(half, 128 * k, 128)].astype(jnp.int32)
@@ -255,9 +280,6 @@
                     got = jnp.take_along_axis(t_ref[t, rows, :], at, axis=1, mode="promise_in_bounds")
                     found = jnp.where(tile == t, got, found)
                 s_ref[half, rows, 128 * k : 128 * k + 128] = found
-            return carry
-
-        lax.fori_loop(0, boards // GROUP, look_up, 0)
         if half is not me:
             sum_copy = to_partner(s_ref.at[1 - me], s_ref.at[2], sum_sem)
 
@@ -277,6 +299,8 @@
         jnp.concatenate([piece for pair in pieces for piece in pair], axis=0), hold, preferred_element_type=F32
     )
     sum_copy.wait()
+    for load in loads[3:]:
+        load.wait()
     part = mass = None
     for k, core in ((0, me), (1, 1 - me)):
         at = 2 * boards * k
@@ -289,14 +313,17 @@
         pot = column(pot_ref[...], core * boards, boards)
         bet = column(bet_ref[...], core * boards, boards)
         half_pot = 0.5 * pot
-        stake = (half_pot / hand_count) * live
-        values = jnp.maximum(((half_pot + bet * pot) / hand_count) * margin, -stake)
+        stake = half_pot * live
+        values = jnp.maximum((half_pot + bet * pot) * margin, -stake)
         values_ref[rows_of(core), :] = values
         values, stake = (jnp.sum(v, axis=0, keepdims=True) for v in (values, stake))
         part = values if part is None else part + values
         mass = stake if mass is None else mass + stake
-    part, mass = part / total_boards, mass / total_boards
-    trav = trav_ref[...]
+    save = pltpu.make_async_copy(values_ref, values_hbm, io_sem.at[6])
+    save.start()
+    scale = 1.0 / (hand_count * total_boards)
+    part, mass = part * scale, mass * scale
+    trav = trav_ref[...].reshape(1, own_count)
     numerator = jnp.sum(part * trav, axis=1, keepdims=True)
     denominator = jnp.sum(mass * trav, axis=1, keepdims=True)
 
@@ -339,6 +366,7 @@
     hand_ref[...] = total
     ends = total[6:7] + rest[6:7]
     ratio_ref[...] = ends[:, 0:1] / ends[:, 1:2]
+    save.wait()
     for copy in sent:
         copy.wait_send()
 
@@ -358,9 +386,17 @@
             jax.ShapeDtypeStruct((8, 128), F32),
             jax.ShapeDtypeStruct((1, 1), F32),
         ),
-        in_specs=[whole] * 6,
-        out_specs=(whole,) * 3,
+        in_specs=[pl.BlockSpec(memory_space=pl.ANY)] * 6,
+        out_specs=(pl.BlockSpec(memory_space=pl.ANY), whole, whole),
         scratch_shapes=[
+            pltpu.VMEM((boards, own_count), BF16),
+            pltpu.VMEM((half, hand_count), jnp.int32),
+            pltpu.VMEM((2, hand_count), jnp.int32),
+            pltpu.VMEM((1, boards), F32),
+            pltpu.VMEM((1, boards), F32),
+            pltpu.VMEM((own_count,), F32),
+            pltpu.VMEM((boards, own_count), F32),
+            pltpu.SemaphoreType.DMA((7,)),
             pltpu.VMEM((8 * half, width), BF16),
             pltpu.VMEM((PARTS, CARDS, ROWS, width), BF16),
             pltpu.VMEM((PARTS, CARDS, ROWS, 8 * half), F32),
@@ -368,8 +404,8 @@
             pltpu.VMEM((CARDS, ROWS, 4 * half), F32),
             pltpu.VMEM((2, CARDS, ROWS, 4 * half), F32),
             pltpu.VMEM((3, half, width), F32),
-            pltpu.VMEM((2, GROUP * HI, width), BF16),
-            pltpu.VMEM((2, GROUP * SLOT, width), BF16),
+            pltpu.VMEM((half // GROUP, GROUP * HI, width), BF16),
+            pltpu.VMEM((half // GROUP, GROUP * SLOT, width), BF16),
             pltpu.VMEM((2, 2 * GROUP * HI, 128), F32),
             pltpu.VMEM((HI // 4, half, 128), F32),
             pltpu.VMEM((3, half, lanes), F32),
@@ -392,8 +428,8 @@
             vmem_limit_bytes=56 * 1024 * 1024, collective_id=0, has_side_effects=True
         ),
         cost_estimate=pl.CostEstimate(flops=10**9, bytes_accessed=10**6, transcendentals=0),
-    )(opp_reach, hand_rank, hand_cards.T, pot[None, :], bet_frac[None, :], trav_reach[None, :])
-    return board_values, hand_rows.reshape(-1)[:own_count], ratio[0, 0]
+    )(opp_reach, hand_rank, hand_cards.T, pot[None, :], bet_frac[None, :], trav_reach)
+    return board_values * (1.0 / hand_count), hand_rows.reshape(-1)[:own_count], ratio[0, 0]
 
 
 def solution(mesh):

time: 39.7 us -> 37.6 us (0.947)
  local copies, waits for them, and re-layouts: 3.47 us -> 0.6 us
  other arithmetic: 0 us -> 1.62 us
  Pallas kernels: 33.6 us -> 32.8 us
    unnamed x6 -> x3, local copies, waits for them, and re-layouts: 2.89 us -> 0.6 us
    mul x0 -> x1, other arithmetic: none -> 1.62 us  [local(): board_values * (1.0 / hand_count)]
    pallas_call x1, Pallas kernels: 33.6 us -> 32.8 us  [local(): pl.pallas_call(functools.partial(fused_kernel, total_boards, hand_count),...]
    broadcast_in_dim x1 -> x0, local copies, waits for them, and re-layouts: 0.58 us -> none  [local(): trav_reach[None, :]]
where the time goes in v4:
time: 37.6 us; the launch traced here: 37.5 us
  Pallas kernels  32.8 us (87%)
  between operations  2.41 us (6%)
  other arithmetic  1.62 us (4%)
  local copies, waits for them, and re-layouts  0.6 us (2%)
    pallas_call x1, Pallas kernels, local(): pl.pallas_call(functools.partial(fused_kernel, total_boards, hand_count),...  32.8 us
    mul x1, other arithmetic, local(): board_values * (1.0 / hand_count)  1.62 us

profile of v4, /device:TPU:1, one launch (start us, length us, event | category | flops | bytes accessed | tf_op | source)
XLA Modules:
  0.0 37.5 jit_solution(6234124907000638461)
XLA Ops:
  0.6 32.8 %shard_map.85 = (f32[64,663]{1,0:T(8,128)}, f32[8,128]{1,0:T(8,128)}, f32[1,1]{1,0:T(1,128)}) custom-call(bf16[64,663]{1,0:T(8,128)(2,1)} %reach_hbm.1, s32[64,1326]{1,0:T(8,128)} %rank_hbm.1, s32[2,1326]{1,0:T(2,128)} %bitcast.7, f32[1,64]{1,0:T(1,128)} %bitcast.8, f32[1,64]{1,0:T(1,128)} %bitcast.9, f32[663]{0:T(1024)} %trav_hbm.1), custom_call_target="tpu_custom_call" | custom-call | flops 1000000000 | bytes 1000000 | tf_op jit(solution)/shard_map/pallas_call | solution.py:382
  33.5 0.0 copy-start
  33.5 1.6 %broadcast_multiply_fusion = f32[64,663]{1,0:T(8,128)} fusion(f32[64,663]{1,0:T(8,128)} %get-tuple-element.6), kind=kLoop, calls=%fused_computation | loop fusion | flops 42432 | bytes 339456 | tf_op jit(solution)/shard_map/mul | solution.py:432
  35.1 0.0 copy-done
  35.1 0.6 %copy.11 = f32[663]{0:T(1024)} copy(f32[663]{0:T(1024)S(1)} %bitcast.6) | data formatting | bytes 5304
Async XLA Ops:
  33.5 1.6 %copy-start = (f32[8,128]{1,0:T(8,128)S(1)}, f32[8,128]{1,0:T(8,128)}, u32[]{:S(2)}) copy-start(f32[8,128]{1,0:T(8,128)} %get-tuple-element.7) | copy-start | bytes 12292

commit v5 on v4

--- a/solution.py
+++ b/solution.py
@@ -42,12 +42,12 @@
     y, x, z, h = places
     plane = [
         {"board_0": lax.rem(y + i, YS), "board_1": lax.rem(x + j, XS)}
-        for i in range(YS)
-        for j in range(XS)
+        for i in (2, 1, 3, 0)
+        for j in (2, 1, 3, 0)
         if i or j
     ]
-    line = [{"board_2": lax.rem(z + i, ZS)} for i in range(1, ZS)]
-    cross = [{"board_2": lax.rem(z + i, ZS), "hand": 1 - h} for i in range(ZS)]
+    line = [{"board_2": lax.rem(z + i, ZS)} for i in (4, 3, 5, 2, 6, 1, 7)]
+    cross = [{"board_2": lax.rem(z + i, ZS), "hand": 1 - h} for i in (4, 3, 5, 2, 6, 1, 7, 0)]
     return plane, line, cross
 
 
@@ -60,11 +60,11 @@
 def fused_kernel(
     total_boards, hand_count,
     reach_hbm, rank_hbm, cards_hbm, pot_hbm, bet_hbm, trav_hbm,
-    values_hbm, hand_ref, ratio_ref,
-    reach_ref, rank_ref, cards_ref, pot_ref, bet_ref, trav_ref, values_ref, io_sem,
-    x_ref, p_ref, o_ref, w_ref, g_ref, q_ref, f_ref, a_ref, b_ref, h_ref, t_ref, s_ref, c_ref, k_ref,
+    values_ref, hand_ref, ratio_ref,
+    reach_ref, rank_ref, cards_ref, pot_ref, bet_ref, trav_ref, io_sem,
+    x_ref, p_ref, o_ref, w_ref, g_ref, q_ref, l_ref, f_ref, a_ref, b_ref, h0_ref, h1_ref, h2_ref, h3_ref, t0_ref, t1_ref, t2_ref, t3_ref, s_ref, c_ref,
     swap_ref, mine_ref, plane_ref, line_ref, cross_ref,
-    swap_sem, pair_sem, total_sem, sum_sem, plane_sem, line_sem, cross_sem,
+    swap_sem, pair_sem, sum_sem, plane_sem, line_sem, cross_sem,
 ):
     all_boards, own_count = reach_ref.shape
     boards = all_boards // 2
@@ -113,21 +113,17 @@
         c_ref[:, start + lanes - 128 : start + lanes] = jnp.full((2, 128), -1.0, F32)
         c_ref[:, start : start + own_count] = cards_ref[:, half * own_count : (half + 1) * own_count].astype(F32)
 
-    row16 = iota((16, width), 0)
+    row16 = iota((16, lanes), 0)
     own_row = [
         jnp.where(row16 < SHARE, row16 + SHARE * q, -5).astype(F32).astype(BF16) for q in range(PARTS)
     ]
 
-    def hot_rows(d, carry):
-        low, high = c_ref[0:1, :], c_ref[1:2, :]
-        df = d.astype(F32)
-        partner = jnp.where(low == df, high, jnp.where(high == df, low, -1.0))
-        wide = jnp.broadcast_to(partner, (16, width)).astype(BF16)
+    def hot_rows(half, d):
+        low, high = c_ref[0:1, cols_of(half)], c_ref[1:2, cols_of(half)]
+        partner = jnp.where(low == float(d), high, jnp.where(high == float(d), low, -1.0))
+        wide = jnp.broadcast_to(partner, (16, lanes)).astype(BF16)
         for q in range(PARTS):
-            p_ref[q, d] = jnp.where(wide == own_row[q], BF16(1), BF16(0))
-        return carry
-
-    lax.fori_loop(0, CARDS, hot_rows, 0)
+            p_ref[d, q, :, cols_of(half)] = jnp.where(wide == own_row[q], BF16(1), BF16(0))
 
     loads[1].wait()
     loads[2].wait()
@@ -149,52 +145,66 @@
         for k in range(1, PARTS):
             x_ref[k * boards : (k + 1) * boards, cols_of(half)] = x_ref[0:boards, cols_of(half)]
 
+    chunk = CARDS // PARTS
+
     def to_cards(half, more):
-        for q in range(PARTS):
-            rows = p_ref[q, :, :, cols_of(half)].reshape(CARDS * ROWS, lanes)
+        for i in range(PARTS):
+            these = slice(chunk * i, chunk * (i + 1))
+            if not more:
+                for d in range(chunk * i, chunk * (i + 1)):
+                    hot_rows(half, d)
+            if more:
+                low_factor(half, i)
+                high_factor(half, i)
+            rows = p_ref[these, :, :, cols_of(half)].reshape(chunk * PARTS * ROWS, lanes)
             got = lax.dot_general(rows, x_ref[:, cols_of(half)], NT, preferred_element_type=F32)
-            got = got.reshape(CARDS, ROWS, 2 * block)
-            o_ref[q] = got + o_ref[q] if more else got
+            got = got.reshape(chunk, PARTS, ROWS, 2 * block)
+            o_ref[these] = got + o_ref[these] if more else got
 
     digit = iota((16, lanes), 0).astype(F32).astype(BF16)
 
-    def high_factor(half):
-        for b in range(boards):
-            hi = jnp.broadcast_to(f_ref[0, b : b + 1, cols_of(half)], (16, lanes)).astype(BF16)
-            reach = jnp.broadcast_to(f_ref[2, b : b + 1, cols_of(half)], (16, lanes)).astype(BF16)
+    def high_factor(half, g):
+        for b in range(GROUP):
+            at = GROUP * g + b
+            hi = jnp.broadcast_to(f_ref[0, at : at + 1, cols_of(half)], (16, lanes)).astype(BF16)
+            reach = jnp.broadcast_to(f_ref[2, at : at + 1, cols_of(half)], (16, lanes)).astype(BF16)
             for part in range(HI // 16):
-                at = HI * (b % GROUP) + 16 * part
+                rows = slice(HI * b + 16 * part, HI * b + 16 * part + 16)
                 hit = hi == digit + BF16(16 * part)
-                a_ref[b // GROUP, at : at + 16, cols_of(half)] = jnp.where(hit, reach, BF16(0))
-
-    def low_factor(half):
-        for b in range(boards):
-            lo = jnp.broadcast_to(f_ref[1, b : b + 1, cols_of(half)], (16, lanes)).astype(BF16)
+                a_ref[g, rows, cols_of(half)] = jnp.where(hit, reach, BF16(0))
+
+    def low_factor(half, g):
+        for b in range(GROUP):
+            at = GROUP * g + b
+            lo = jnp.broadcast_to(f_ref[1, at : at + 1, cols_of(half)], (16, lanes)).astype(BF16)
             for part in range(SLOT // 16):
-                at = 128 * (b % 2) + (128 - SLOT // 2 * (b % GROUP) + 16 * part) % 128
-                b_ref[b // GROUP, at : at + 16, cols_of(half)] = lax.clamp(
+                at = 128 * (b % 2) + (128 - SLOT // 2 * b + 16 * part) % 128
+                b_ref[g, at : at + 16, cols_of(half)] = lax.clamp(
                     BF16(-1), digit + BF16(16 * part) - lo, BF16(1)
                 )
 
     place(me, reach_ref[rows_of(me), :])
     to_cards(me, False)
+    loads[3].wait()
+    for d in range(CARDS):
+        hot_rows(1 - me, d)
     pl.semaphore_wait(barrier, len(plane + line + cross))
     swap = to_partner(reach_ref.at[rows_of(1 - me), :], swap_ref, swap_sem)
-    low_factor(0)
-    low_factor(1)
-    high_factor(me)
+    groups = boards // GROUP
+    for g in range(groups):
+        low_factor(me, g)
+        high_factor(me, g)
     swap.wait()
     place(1 - me, swap_ref[...])
-    high_factor(1 - me)
     to_cards(1 - me, True)
 
     part_of = iota((ROWS, block), 1) // boards
 
     def pack(d, carry):
         for ref, at in ((w_ref, 0), (g_ref, block)):
-            got = o_ref[0, d, :, at : at + block]
+            got = o_ref[d, 0, :, at : at + block]
             for q in range(1, PARTS):
-                got = jnp.where(part_of == q, o_ref[q, d, :, at : at + block], got)
+                got = jnp.where(part_of == q, o_ref[d, q, :, at : at + block], got)
             ref[d] = got
         return carry
 
@@ -210,12 +220,10 @@
                 term = sign.astype(F32) * we.astype(F32)
                 sums[k] = term if sums[k] is None else sums[k] + term
         for k in range(DBLOCK):
-            q_ref[0, DBLOCK * i + k] = sums[k]
+            q_ref[DBLOCK * i + k] = sums[k]
         return carry
 
     lax.fori_loop(0, CARDS // DBLOCK, pairs, 0)
-    pair_copy = to_partner(q_ref.at[0], q_ref.at[1], pair_sem)
-
     card = iota((64, lanes), 0).astype(F32)
     card_totals = jnp.zeros((boards, 64), F32)
     for half in (1 - me, me):
@@ -223,53 +231,68 @@
         card_totals = card_totals + lax.dot_general(
             x_ref[0:boards, cols_of(half)], hold, NT, preferred_element_type=F32
         )
-    k_ref[0] = jnp.concatenate([card_totals, jnp.zeros((boards, 64), F32)], axis=1)
-    total_copy = to_partner(k_ref.at[0], k_ref.at[1], total_sem)
+    wide = jnp.concatenate([card_totals, jnp.zeros((boards, 64), F32)], axis=1)
+    pair_lanes = PARTS * CARDS * ROWS
+    turned = jnp.transpose(q_ref[...].reshape(CARDS * ROWS, block))
+    for k, piece in enumerate(split2(turned)):
+        for q in range(PARTS):
+            l_ref[0, boards * k : boards * (k + 1), CARDS * ROWS * q : CARDS * ROWS * (q + 1)] = piece[
+                boards * q : boards * (q + 1)
+            ]
+    for k, piece in enumerate(split2(wide)):
+        l_ref[0, boards * k : boards * (k + 1), pair_lanes:] = piece
+    pair_copy = to_partner(l_ref.at[0], l_ref.at[1], pair_sem)
 
     even = iota((GROUP, 128), 0) % 2 == 0
     slot = ((iota((GROUP, 128), 1) + SLOT // 2 * iota((GROUP, 128), 0)) % 128) // SLOT
     tiles = HI // 4
-    for g in range(boards // GROUP):
-        now = g % 2
+    h_refs = (h0_ref, h1_ref, h2_ref, h3_ref)
+    t_refs = (t0_ref, t1_ref, t2_ref, t3_ref)
+
+    def tabulate(g):
         got = lax.dot_general(a_ref[g], b_ref[g], NT, preferred_element_type=F32)
-        h_ref[now, 0 : GROUP * HI, :] = got[:, 0:128]
-        h_ref[now, GROUP * HI :, :] = got[:, 128:256]
+        h_refs[g][0 : GROUP * HI, :] = got[:, 0:128]
+        h_refs[g][GROUP * HI :, :] = got[:, 128:256]
+
+    def lay_out(g):
         for t in range(tiles):
             row = None
             for k in range(4):
                 at = 4 * t + k
                 part = jnp.where(
                     even,
-                    h_ref[now, pl.ds(at, GROUP, stride=HI), :],
-                    h_ref[now, pl.ds(at + GROUP * HI, GROUP, stride=HI), :],
+                    h_refs[g][pl.ds(at, GROUP, stride=HI), :],
+                    h_refs[g][pl.ds(at + GROUP * HI, GROUP, stride=HI), :],
                 )
                 part = pltpu.roll(part, SLOT * k, 1) if k else part
                 row = part if row is None else jnp.where(slot == k, part, row)
-            t_ref[t, GROUP * g : GROUP * (g + 1), :] = pltpu.roll(row, 0, 1, stride=SLOT // 2, stride_axis=0)
-
-    spot = iota((boards, 128), 1) % SLOT == LO
-    below = []
-    run = jnp.zeros((boards, 128), F32)
-    whole = []
-    for t in range(tiles):
-        mark = jnp.where(spot, t_ref[t], 0.0)
-        whole.append(mark)
-        below.append(run)
-        run = run + mark
+            t_refs[g][t] = pltpu.roll(row, 0, 1, stride=SLOT // 2, stride_axis=0)
+
     src, dst = iota((256, 128), 0), iota((256, 128), 1)
     within = (dst // SLOT > (src - 128) // SLOT).astype(F32) - (dst // SLOT < (src - 128) // SLOT).astype(F32)
     spread = jnp.where(src % SLOT == LO, jnp.where(src < 128, 1.0, within), 0.0).astype(BF16)
-    both = jnp.concatenate(
-        [jnp.concatenate([below[t] - (run - below[t] - whole[t]), whole[t]], axis=1) for t in range(tiles)], axis=0
-    )
-    high, low = split2(both)
-    got = jnp.dot(high, spread, preferred_element_type=F32) + jnp.dot(low, spread, preferred_element_type=F32)
-    for t in range(tiles):
-        t_ref[t] = t_ref[t] + got[boards * t : boards * (t + 1)]
-
-    for half in (1 - me, me):
-        for g in range(boards // GROUP):
-            rows = slice(GROUP * g, GROUP * (g + 1))
+    spot = iota((GROUP, 128), 1) % SLOT == LO
+
+    def add_rows(g):
+        run = jnp.zeros((GROUP, 128), F32)
+        below, whole = [], []
+        for t in range(tiles):
+            mark = jnp.where(spot, t_refs[g][t], 0.0)
+            whole.append(mark)
+            below.append(run)
+            run = run + mark
+        both = jnp.concatenate(
+            [jnp.concatenate([below[t] - (run - below[t] - whole[t]), whole[t]], axis=1) for t in range(tiles)],
+            axis=0,
+        )
+        got = jnp.dot(jnp.concatenate(split2(both), axis=0), spread, preferred_element_type=F32)
+        got = got[: GROUP * tiles] + got[GROUP * tiles :]
+        for t in range(tiles):
+            t_refs[g][t] = t_refs[g][t] + got[GROUP * t : GROUP * (t + 1)]
+
+    def look_up(g):
+        rows = slice(GROUP * g, GROUP * (g + 1))
+        for half in (1 - me, me):
             for k in range(lanes // 128):
                 hi = f_ref[0, rows, cols_of(half, 128 * k, 128)].astype(jnp.int32)
                 lo = f_ref[1, rows, cols_of(half, 128 * k, 128)].astype(jnp.int32)
@@ -277,35 +300,35 @@
                 at = ((hi & 3) << 5) + lo
                 found = jnp.zeros((GROUP, 128), F32)
                 for t in range(tiles):
-                    got = jnp.take_along_axis(t_ref[t, rows, :], at, axis=1, mode="promise_in_bounds")
+                    got = jnp.take_along_axis(t_refs[g][t], at, axis=1, mode="promise_in_bounds")
                     found = jnp.where(tile == t, got, found)
                 s_ref[half, rows, 128 * k : 128 * k + 128] = found
-        if half is not me:
-            sum_copy = to_partner(s_ref.at[1 - me], s_ref.at[2], sum_sem)
+
+    stages = (tabulate, lay_out, add_rows, look_up)
+    for step in range(groups + len(stages) - 1):
+        for k, stage in enumerate(stages):
+            if 0 <= step - k < groups:
+                stage(step - k)
+    sum_copy = to_partner(s_ref.at[1 - me], s_ref.at[2], sum_sem)
 
     pair_copy.wait()
-    total_copy.wait()
-    turned = [jnp.transpose(q_ref[k].reshape(CARDS * ROWS, block)) for k in range(2)]
-    shared = jnp.zeros((4 * boards, lanes), F32)
-    for q in range(PARTS):
-        pieces = [split2(t[boards * q : boards * (q + 1)]) for t in turned]
-        shared = shared + jnp.dot(
-            jnp.concatenate([piece for pair in pieces for piece in pair], axis=0),
-            p_ref[q, :, :, cols_of(me)].reshape(CARDS * ROWS, lanes),
-            preferred_element_type=F32,
-        )
-    pieces = [split2(k_ref[k][:, 0:64]) for k in range(2)]
+    back = [p_ref[:, q, :, cols_of(me)].reshape(CARDS * ROWS, lanes) for q in range(PARTS)]
+    shared = jnp.dot(
+        l_ref[:, :, 0:pair_lanes].reshape(4 * boards, pair_lanes),
+        jnp.concatenate(back, axis=0),
+        preferred_element_type=F32,
+    )
     held = jnp.dot(
-        jnp.concatenate([piece for pair in pieces for piece in pair], axis=0), hold, preferred_element_type=F32
+        l_ref[:, :, pair_lanes:].reshape(4 * boards, 128)[:, 0:64], hold, preferred_element_type=F32
     )
     sum_copy.wait()
-    for load in loads[3:]:
+    for load in loads[4:]:
         load.wait()
     part = mass = None
     for k, core in ((0, me), (1, 1 - me)):
         at = 2 * boards * k
         live = (
-            0.5 * jnp.sum(k_ref[k][:, 0:64], axis=1, keepdims=True)
+            0.5 * jnp.sum(l_ref[k, :, pair_lanes:].astype(F32).reshape(2, boards, 128).sum(0), axis=1, keepdims=True)
             - (held[at : at + boards] + held[at + boards : at + 2 * boards])
         )[:, 0:own_count] + reach_ref[rows_of(core), :].astype(F32)
         sums = s_ref[me] if k == 0 else s_ref[2]
@@ -313,16 +336,14 @@
         pot = column(pot_ref[...], core * boards, boards)
         bet = column(bet_ref[...], core * boards, boards)
         half_pot = 0.5 * pot
+        half_pot, bet = half_pot / hand_count, bet / hand_count
         stake = half_pot * live
         values = jnp.maximum((half_pot + bet * pot) * margin, -stake)
         values_ref[rows_of(core), :] = values
         values, stake = (jnp.sum(v, axis=0, keepdims=True) for v in (values, stake))
         part = values if part is None else part + values
         mass = stake if mass is None else mass + stake
-    save = pltpu.make_async_copy(values_ref, values_hbm, io_sem.at[6])
-    save.start()
-    scale = 1.0 / (hand_count * total_boards)
-    part, mass = part * scale, mass * scale
+    part, mass = part / total_boards, mass / total_boards
     trav = trav_ref[...].reshape(1, own_count)
     numerator = jnp.sum(part * trav, axis=1, keepdims=True)
     denominator = jnp.sum(mass * trav, axis=1, keepdims=True)
@@ -366,9 +387,28 @@
     hand_ref[...] = total
     ends = total[6:7] + rest[6:7]
     ratio_ref[...] = ends[:, 0:1] / ends[:, 1:2]
-    save.wait()
     for copy in sent:
         copy.wait_send()
+
+
+def write_kernel(*refs):
+    count = (len(refs) - 1) // 2
+    copies = [pltpu.make_async_copy(refs[k], refs[count + k], refs[-1].at[k]) for k in range(count)]
+    for copy in copies:
+        copy.start()
+    for copy in copies:
+        copy.wait()
+
+
+def write_out(*arrays):
+    return pl.pallas_call(
+        write_kernel,
+        out_shape=tuple(jax.ShapeDtypeStruct(a.shape, a.dtype) for a in arrays),
+        in_specs=[pl.BlockSpec(memory_space=pltpu.VMEM)] * len(arrays),
+        out_specs=(pl.BlockSpec(memory_space=pl.ANY),) * len(arrays),
+        scratch_shapes=[pltpu.SemaphoreType.DMA((len(arrays),))],
+        cost_estimate=pl.CostEstimate(flops=10**6, bytes_accessed=10**6, transcendentals=0),
+    )(*(pltpu.with_memory_space_constraint(a, pltpu.VMEM) for a in arrays))
 
 
 def local(opp_reach, hand_rank, hand_cards, pot, bet_frac, trav_reach):
@@ -382,12 +422,12 @@
     board_values, hand_rows, ratio = pl.pallas_call(
         functools.partial(fused_kernel, total_boards, hand_count),
         out_shape=(
-            jax.ShapeDtypeStruct((boards, own_count), F32),
-            jax.ShapeDtypeStruct((8, 128), F32),
-            jax.ShapeDtypeStruct((1, 1), F32),
+            pltpu.VMEM((boards, own_count), F32),
+            pltpu.VMEM((8, 128), F32),
+            pltpu.VMEM((1, 1), F32),
         ),
         in_specs=[pl.BlockSpec(memory_space=pl.ANY)] * 6,
-        out_specs=(pl.BlockSpec(memory_space=pl.ANY), whole, whole),
+        out_specs=(whole, whole, whole),
         scratch_shapes=[
             pltpu.VMEM((boards, own_count), BF16),
             pltpu.VMEM((half, hand_count), jnp.int32),
@@ -395,28 +435,26 @@
             pltpu.VMEM((1, boards), F32),
             pltpu.VMEM((1, boards), F32),
             pltpu.VMEM((own_count,), F32),
-            pltpu.VMEM((boards, own_count), F32),
-            pltpu.SemaphoreType.DMA((7,)),
+            pltpu.SemaphoreType.DMA((6,)),
             pltpu.VMEM((8 * half, width), BF16),
-            pltpu.VMEM((PARTS, CARDS, ROWS, width), BF16),
-            pltpu.VMEM((PARTS, CARDS, ROWS, 8 * half), F32),
+            pltpu.VMEM((CARDS, PARTS, ROWS, width), BF16),
+            pltpu.VMEM((CARDS, PARTS, ROWS, 8 * half), F32),
             pltpu.VMEM((CARDS, ROWS, 4 * half), F32),
             pltpu.VMEM((CARDS, ROWS, 4 * half), F32),
-            pltpu.VMEM((2, CARDS, ROWS, 4 * half), F32),
+            pltpu.VMEM((CARDS, ROWS, 4 * half), F32),
+            pltpu.VMEM((2, 2 * half, PARTS * CARDS * ROWS + 128), BF16),
             pltpu.VMEM((3, half, width), F32),
             pltpu.VMEM((half // GROUP, GROUP * HI, width), BF16),
             pltpu.VMEM((half // GROUP, GROUP * SLOT, width), BF16),
-            pltpu.VMEM((2, 2 * GROUP * HI, 128), F32),
-            pltpu.VMEM((HI // 4, half, 128), F32),
+            *[pltpu.VMEM((2 * GROUP * HI, 128), F32)] * 4,
+            *[pltpu.VMEM((HI // 4, GROUP, 128), F32)] * 4,
             pltpu.VMEM((3, half, lanes), F32),
             pltpu.VMEM((2, width), F32),
-            pltpu.VMEM((2, half, 128), F32),
             pltpu.VMEM((half, own_count), BF16),
             pltpu.VMEM((2, 8, 128), F32),
             pltpu.VMEM((YS * XS, 8, 128), F32),
             pltpu.VMEM((ZS, 8, 128), F32),
             pltpu.VMEM((ZS, 8, 128), F32),
-            pltpu.SemaphoreType.DMA((2,)),
             pltpu.SemaphoreType.DMA((2,)),
             pltpu.SemaphoreType.DMA((2,)),
             pltpu.SemaphoreType.DMA((2,)),
@@ -429,7 +467,8 @@
         ),
         cost_estimate=pl.CostEstimate(flops=10**9, bytes_accessed=10**6, transcendentals=0),
     )(opp_reach, hand_rank, hand_cards.T, pot[None, :], bet_frac[None, :], trav_reach)
-    return board_values * (1.0 / hand_count), hand_rows.reshape(-1)[:own_count], ratio[0, 0]
+    board_values, hand_rows, ratio = write_out(board_values, hand_rows, ratio)
+    return board_values, hand_rows.reshape(-1)[:own_count], ratio[0, 0]
 
 
 def solution(mesh):

time: 37.6 us -> 33.6 us (0.89)
  between operations: 2.41 us -> 0.64 us
  other arithmetic: 1.62 us -> 0 us
  local copies, waits for them, and re-layouts: 0.6 us -> 0 us
    mul x1 -> x0, other arithmetic: 1.62 us -> none  [local(): board_values * (1.0 / hand_count)]
    pallas_call x1, Pallas kernels: 32.8 us -> 31.4 us  [local(): pl.pallas_call(functools.partial(fused_kernel, total_boards, hand_count),...]
    pallas_call x0 -> x1, Pallas kernels: none -> 1.34 us  [write_out(): pl.pallas_call(write_kernel, out_shape=tuple((jax.ShapeDtypeStruct(a.shap...]
    unnamed x3 -> x0, local copies, waits for them, and re-layouts: 0.6 us -> none
where the time goes in v5:
time: 33.6 us; the launch traced here: 33.4 us
  Pallas kernels  32.8 us (98%)
  between operations  0.64 us (2%)
    pallas_call x1, Pallas kernels, local(): pl.pallas_call(functools.partial(fused_kernel, total_boards, hand_count),...  31.4 us
    pallas_call x1, Pallas kernels, write_out(): pl.pallas_call(write_kernel, out_shape=tuple((jax.ShapeDtypeStruct(a.shap...  1.34 us

profile of v5, /device:TPU:1, one launch (start us, length us, event | category | flops | bytes accessed | tf_op | source)
XLA Modules:
  0.0 33.4 jit_solution(10088181759589769066)
XLA Ops:
  0.6 31.4 %shard_map.85 = (f32[64,663]{1,0:T(8,128)S(1)}, f32[8,128]{1,0:T(8,128)S(1)}, f32[1,1]{1,0:T(1,128)}) custom-call(bf16[64,663]{1,0:T(8,128)(2,1)} %reach_hbm.1, s32[64,1326]{1,0:T(8,128)} %rank_hbm.1, s32[2,1326]{1,0:T(2,128)} %bitcast.6, f32[1,64]{1,0:T(1,128)} %bitcast.8, f32[1,64]{1,0:T(1,128)} %bitcast.9, f32[663]{0:T(1024)} %trav_hbm.1), custom_call_target="tpu_custom_call" | custom-call | flops 1000000000 | bytes 1000000 | tf_op jit(solution)/shard_map/pallas_call | solution.py:422
  32.1 1.3 %shard_map.86 = (f32[64,663]{1,0:T(8,128)}, f32[8,128]{1,0:T(8,128)}, f32[1,1]{1,0:T(1,128)}) custom-call(f32[64,663]{1,0:T(8,128)S(1)} %get-tuple-element.9.refs_0_, f32[8,128]{1,0:T(8,128)S(1)} %get-tuple-element.10.refs_1_, f32[1,1]{1,0:T(1,128)} %get-tuple-element.11.refs_2_), custom_call_target="tpu_custom_call" | custom-call | flops 1000000 | bytes 1000000 | tf_op jit(solution)/shard_map/pallas_call | solution.py:404

commit v6 on v5

--- a/solution.py
+++ b/solution.py
@@ -154,7 +154,6 @@
                 for d in range(chunk * i, chunk * (i + 1)):
                     hot_rows(half, d)
             if more:
-                low_factor(half, i)
                 high_factor(half, i)
             rows = p_ref[these, :, :, cols_of(half)].reshape(chunk * PARTS * ROWS, lanes)
             got = lax.dot_general(rows, x_ref[:, cols_of(half)], NT, preferred_element_type=F32)
@@ -178,7 +177,7 @@
             at = GROUP * g + b
             lo = jnp.broadcast_to(f_ref[1, at : at + 1, cols_of(half)], (16, lanes)).astype(BF16)
             for part in range(SLOT // 16):
-                at = 128 * (b % 2) + (128 - SLOT // 2 * b + 16 * part) % 128
+                at = SLOT * b + 16 * part
                 b_ref[g, at : at + 16, cols_of(half)] = lax.clamp(
                     BF16(-1), digit + BF16(16 * part) - lo, BF16(1)
                 )
@@ -194,6 +193,7 @@
     for g in range(groups):
         low_factor(me, g)
         high_factor(me, g)
+        low_factor(1 - me, g)
     swap.wait()
     place(1 - me, swap_ref[...])
     to_cards(1 - me, True)
@@ -208,7 +208,7 @@
             ref[d] = got
         return carry
 
-    lax.fori_loop(0, CARDS, pack, 0)
+    lax.fori_loop(0, CARDS, pack, 0, unroll=4)
 
     def pairs(i, carry):
         mine = [g_ref[DBLOCK * i + k].astype(BF16) for k in range(DBLOCK)]
@@ -243,8 +243,9 @@
         l_ref[0, boards * k : boards * (k + 1), pair_lanes:] = piece
     pair_copy = to_partner(l_ref.at[0], l_ref.at[1], pair_sem)
 
-    even = iota((GROUP, 128), 0) % 2 == 0
-    slot = ((iota((GROUP, 128), 1) + SLOT // 2 * iota((GROUP, 128), 0)) % 128) // SLOT
+    row_slot = iota((GROUP, 128), 0) % 4
+    upper = iota((GROUP, 128), 0) < 4
+    shift = (iota((GROUP, 128), 1) // SLOT - row_slot) % 4
     tiles = HI // 4
     h_refs = (h0_ref, h1_ref, h2_ref, h3_ref)
     t_refs = (t0_ref, t1_ref, t2_ref, t3_ref)
@@ -256,17 +257,21 @@
 
     def lay_out(g):
         for t in range(tiles):
+            parts = [
+                jnp.where(
+                    upper,
+                    h_refs[g][pl.ds(4 * t + k, GROUP, stride=HI), :],
+                    h_refs[g][pl.ds(4 * t + k + GROUP * HI, GROUP, stride=HI), :],
+                )
+                for k in range(4)
+            ]
             row = None
             for k in range(4):
-                at = 4 * t + k
-                part = jnp.where(
-                    even,
-                    h_refs[g][pl.ds(at, GROUP, stride=HI), :],
-                    h_refs[g][pl.ds(at + GROUP * HI, GROUP, stride=HI), :],
-                )
-                part = pltpu.roll(part, SLOT * k, 1) if k else part
-                row = part if row is None else jnp.where(slot == k, part, row)
-            t_refs[g][t] = pltpu.roll(row, 0, 1, stride=SLOT // 2, stride_axis=0)
+                moved = parts[(3 + k) % 4]
+                for p in range(3):
+                    moved = jnp.where(row_slot == p, parts[(p + k) % 4], moved)
+                row = moved if row is None else jnp.where(shift == k, pltpu.roll(moved, SLOT * k, 1), row)
+            t_refs[g][t] = row
 
     src, dst = iota((256, 128), 0), iota((256, 128), 1)
     within = (dst // SLOT > (src - 128) // SLOT).astype(F32) - (dst // SLOT < (src - 128) // SLOT).astype(F32)
@@ -290,19 +295,18 @@
         for t in range(tiles):
             t_refs[g][t] = t_refs[g][t] + got[GROUP * t : GROUP * (t + 1)]
 
-    def look_up(g):
+    def look_up(g, half=1 - me):
         rows = slice(GROUP * g, GROUP * (g + 1))
-        for half in (1 - me, me):
-            for k in range(lanes // 128):
-                hi = f_ref[0, rows, cols_of(half, 128 * k, 128)].astype(jnp.int32)
-                lo = f_ref[1, rows, cols_of(half, 128 * k, 128)].astype(jnp.int32)
-                tile = hi >> 2
-                at = ((hi & 3) << 5) + lo
-                found = jnp.zeros((GROUP, 128), F32)
-                for t in range(tiles):
-                    got = jnp.take_along_axis(t_refs[g][t], at, axis=1, mode="promise_in_bounds")
-                    found = jnp.where(tile == t, got, found)
-                s_ref[half, rows, 128 * k : 128 * k + 128] = found
+        for k in range(lanes // 128):
+            hi = f_ref[0, rows, cols_of(half, 128 * k, 128)].astype(jnp.int32)
+            lo = f_ref[1, rows, cols_of(half, 128 * k, 128)].astype(jnp.int32)
+            tile = hi >> 2
+            at = ((hi & 3) << 5) + lo
+            found = jnp.zeros((GROUP, 128), F32)
+            for t in range(tiles):
+                got = jnp.take_along_axis(t_refs[g][t], at, axis=1, mode="promise_in_bounds")
+                found = jnp.where(tile == t, got, found)
+            s_ref[half, rows, 128 * k : 128 * k + 128] = found
 
     stages = (tabulate, lay_out, add_rows, look_up)
     for step in range(groups + len(stages) - 1):
@@ -312,6 +316,8 @@
     sum_copy = to_partner(s_ref.at[1 - me], s_ref.at[2], sum_sem)
 
     pair_copy.wait()
+    for g in range(groups):
+        look_up(g, me)
     back = [p_ref[:, q, :, cols_of(me)].reshape(CARDS * ROWS, lanes) for q in range(PARTS)]
     shared = jnp.dot(
         l_ref[:, :, 0:pair_lanes].reshape(4 * boards, pair_lanes),

time: 33.6 us -> 32.6 us (0.970)
  Pallas kernels: 32.8 us -> 31.8 us
    pallas_call x1, Pallas kernels: 31.4 us -> 30.5 us  [local(): pl.pallas_call(functools.partial(fused_kernel, total_boards, hand_count),...]
where the time goes in v6:
time: 32.6 us; the launch traced here: 32.5 us
  Pallas kernels  31.8 us (98%)
  between operations  0.64 us (2%)
    pallas_call x1, Pallas kernels, local(): pl.pallas_call(functools.partial(fused_kernel, total_boards, hand_count),...  30.5 us
    pallas_call x1, Pallas kernels, write_out(): pl.pallas_call(write_kernel, out_shape=tuple((jax.ShapeDtypeStruct(a.shap...  1.34 us

profile of v6, /device:TPU:1, one launch (start us, length us, event | category | flops | bytes accessed | tf_op | source)
XLA Modules:
  0.0 32.5 jit_solution(18192496299163394999)
XLA Ops:
  0.6 30.5 %shard_map.85 = (f32[64,663]{1,0:T(8,128)S(1)}, f32[8,128]{1,0:T(8,128)S(1)}, f32[1,1]{1,0:T(1,128)}) custom-call(bf16[64,663]{1,0:T(8,128)(2,1)} %reach_hbm.1, s32[64,1326]{1,0:T(8,128)} %rank_hbm.1, s32[2,1326]{1,0:T(2,128)} %bitcast.6, f32[1,64]{1,0:T(1,128)} %bitcast.8, f32[1,64]{1,0:T(1,128)} %bitcast.9, f32[663]{0:T(1024)} %trav_hbm.1), custom_call_target="tpu_custom_call" | custom-call | flops 1000000000 | bytes 1000000 | tf_op jit(solution)/shard_map/pallas_call | solution.py:428
  31.1 1.3 %shard_map.86 = (f32[64,663]{1,0:T(8,128)}, f32[8,128]{1,0:T(8,128)}, f32[1,1]{1,0:T(1,128)}) custom-call(f32[64,663]{1,0:T(8,128)S(1)} %get-tuple-element.9.refs_0_, f32[8,128]{1,0:T(8,128)S(1)} %get-tuple-element.10.refs_1_, f32[1,1]{1,0:T(1,128)} %get-tuple-element.11.refs_2_), custom_call_target="tpu_custom_call" | custom-call | flops 1000000 | bytes 1000000 | tf_op jit(solution)/shard_map/pallas_call | solution.py:410

commit v7 on v6

--- a/solution.py
+++ b/solution.py
@@ -20,6 +20,7 @@
 SLOT = 32
 GROUP = 8
 DBLOCK = 4
+WRITES = 4
 YS, XS, ZS = 4, 4, 8
 MESH = pl.DeviceIdType.MESH
 NT = (((1,), (1,)), ((), ()))
@@ -182,18 +183,30 @@
                     BF16(-1), digit + BF16(16 * part) - lo, BF16(1)
                 )
 
+    h_refs = (h0_ref, h1_ref, h2_ref, h3_ref)
+
+    def tabulate(g, half=1 - me):
+        got = lax.dot_general(
+            a_ref[g, :, cols_of(half)], b_ref[g, :, cols_of(half)], NT, preferred_element_type=F32
+        )
+        for k in range(2):
+            rows, piece = slice(GROUP * HI * k, GROUP * HI * (k + 1)), got[:, 128 * k : 128 * (k + 1)]
+            h_refs[g][rows, :] = piece if half is me else piece + h_refs[g][rows, :]
+
     place(me, reach_ref[rows_of(me), :])
     to_cards(me, False)
     loads[3].wait()
+    groups = boards // GROUP
     for d in range(CARDS):
         hot_rows(1 - me, d)
+    for g in range(groups):
+        low_factor(me, g)
+        low_factor(1 - me, g)
     pl.semaphore_wait(barrier, len(plane + line + cross))
     swap = to_partner(reach_ref.at[rows_of(1 - me), :], swap_ref, swap_sem)
-    groups = boards // GROUP
     for g in range(groups):
-        low_factor(me, g)
         high_factor(me, g)
-        low_factor(1 - me, g)
+        tabulate(g, me)
     swap.wait()
     place(1 - me, swap_ref[...])
     to_cards(1 - me, True)
@@ -247,13 +260,7 @@
     upper = iota((GROUP, 128), 0) < 4
     shift = (iota((GROUP, 128), 1) // SLOT - row_slot) % 4
     tiles = HI // 4
-    h_refs = (h0_ref, h1_ref, h2_ref, h3_ref)
     t_refs = (t0_ref, t1_ref, t2_ref, t3_ref)
-
-    def tabulate(g):
-        got = lax.dot_general(a_ref[g], b_ref[g], NT, preferred_element_type=F32)
-        h_refs[g][0 : GROUP * HI, :] = got[:, 0:128]
-        h_refs[g][GROUP * HI :, :] = got[:, 128:256]
 
     def lay_out(g):
         for t in range(tiles):
@@ -399,7 +406,12 @@
 
 def write_kernel(*refs):
     count = (len(refs) - 1) // 2
-    copies = [pltpu.make_async_copy(refs[k], refs[count + k], refs[-1].at[k]) for k in range(count)]
+    pieces = []
+    for source, target in zip(refs[:count], refs[count:-1]):
+        step = max(source.shape[0] // WRITES // 8 * 8, min(source.shape[0], 8))
+        for start in range(0, source.shape[0], step):
+            pieces.append((source.at[start : start + step, :], target.at[start : start + step, :]))
+    copies = [pltpu.make_async_copy(*piece, refs[-1].at[k]) for k, piece in enumerate(pieces)]
     for copy in copies:
         copy.start()
     for copy in copies:
@@ -412,7 +424,7 @@
         out_shape=tuple(jax.ShapeDtypeStruct(a.shape, a.dtype) for a in arrays),
         in_specs=[pl.BlockSpec(memory_space=pltpu.VMEM)] * len(arrays),
         out_specs=(pl.BlockSpec(memory_space=pl.ANY),) * len(arrays),
-        scratch_shapes=[pltpu.SemaphoreType.DMA((len(arrays),))],
+        scratch_shapes=[pltpu.SemaphoreType.DMA((WRITES + len(arrays),))],
         cost_estimate=pl.CostEstimate(flops=10**6, bytes_accessed=10**6, transcendentals=0),
     )(*(pltpu.with_memory_space_constraint(a, pltpu.VMEM) for a in arrays))
 

time: 32.6 us -> 32.6 us (level)
  no operation moved by 1% of the time
where the time goes in v7:
time: 32.6 us; the launch traced here: 32.4 us
  Pallas kernels  31.8 us (98%)
  between operations  0.64 us (2%)
    pallas_call x1, Pallas kernels, local(): pl.pallas_call(functools.partial(fused_kernel, total_boards, hand_count),...  30.4 us
    pallas_call x1, Pallas kernels, write_out(): pl.pallas_call(write_kernel, out_shape=tuple((jax.ShapeDtypeStruct(a.shap...  1.37 us

profile of v7, /device:TPU:1, one launch (start us, length us, event | category | flops | bytes accessed | tf_op | source)
XLA Modules:
  0.0 32.4 jit_solution(12668335521285249749)
XLA Ops:
  0.6 30.4 %shard_map.85 = (f32[64,663]{1,0:T(8,128)S(1)}, f32[8,128]{1,0:T(8,128)S(1)}, f32[1,1]{1,0:T(1,128)}) custom-call(bf16[64,663]{1,0:T(8,128)(2,1)} %reach_hbm.1, s32[64,1326]{1,0:T(8,128)} %rank_hbm.1, s32[2,1326]{1,0:T(2,128)} %bitcast.6, f32[1,64]{1,0:T(1,128)} %bitcast.8, f32[1,64]{1,0:T(1,128)} %bitcast.9, f32[663]{0:T(1024)} %trav_hbm.1), custom_call_target="tpu_custom_call" | custom-call | flops 1000000000 | bytes 1000000 | tf_op jit(solution)/shard_map/pallas_call | solution.py:440
  31.0 1.4 %shard_map.86 = (f32[64,663]{1,0:T(8,128)}, f32[8,128]{1,0:T(8,128)}, f32[1,1]{1,0:T(1,128)}) custom-call(f32[64,663]{1,0:T(8,128)S(1)} %get-tuple-element.9.refs_0_, f32[8,128]{1,0:T(8,128)S(1)} %get-tuple-element.10.refs_1_, f32[1,1]{1,0:T(1,128)} %get-tuple-element.11.refs_2_), custom_call_target="tpu_custom_call" | custom-call | flops 1000000 | bytes 1000000 | tf_op jit(solution)/shard_map/pallas_call | solution.py:422

commit v8 on v7

--- a/solution.py
+++ b/solution.py
@@ -244,6 +244,8 @@
         card_totals = card_totals + lax.dot_general(
             x_ref[0:boards, cols_of(half)], hold, NT, preferred_element_type=F32
         )
+    tabulate(0)
+    tabulate(1)
     wide = jnp.concatenate([card_totals, jnp.zeros((boards, 64), F32)], axis=1)
     pair_lanes = PARTS * CARDS * ROWS
     turned = jnp.transpose(q_ref[...].reshape(CARDS * ROWS, block))
@@ -318,7 +320,7 @@
     stages = (tabulate, lay_out, add_rows, look_up)
     for step in range(groups + len(stages) - 1):
         for k, stage in enumerate(stages):
-            if 0 <= step - k < groups:
+            if 0 <= step - k < groups and (k or step > 1):
                 stage(step - k)
     sum_copy = to_partner(s_ref.at[1 - me], s_ref.at[2], sum_sem)
 
@@ -362,44 +364,52 @@
     denominator = jnp.sum(mass * trav, axis=1, keepdims=True)
 
     spot = XS * y + x
-    mine_ref[0] = jnp.zeros((8, 128), F32)
-    for k in range(lanes // 128):
-        size = min(128, own_count - 128 * k)
-        mine_ref[0, k : k + 1, 0:size] = part[:, 128 * k : 128 * k + size]
-    mine_ref[0, 6:7, :] = jnp.where(iota((1, 128), 1) == 0, numerator, denominator)
+    last = lanes // 128 - 1
+    for k in range(last):
+        mine_ref[0, k : k + 1, :] = part[:, 128 * k : 128 * (k + 1)]
+    fill = jnp.concatenate([part[:, 128 * last :], jnp.zeros((1, lanes - own_count), F32)], axis=1)
+    lane = iota((1, 128), 1)
+    mine_ref[0, last : last + 1, :] = jnp.where(lane == 126, numerator, jnp.where(lane == 127, denominator, fill))
+
+    rows, ends_row = slice(0, lanes // 128), slice(last, last + 1)
 
     def exchange(source, groups):
         sent = []
-        for peers, here, slots, sems in groups:
+        for peers, here, these, slots, sems in groups:
             for k, peer in enumerate(peers):
                 copy = pltpu.make_async_remote_copy(
-                    source, slots.at[here], sems.at[0, k], sems.at[1, here], device_id=peer, device_id_type=MESH
+                    source.at[these, :], slots.at[here, these, :], sems.at[0, k], sems.at[1, here],
+                    device_id=peer, device_id_type=MESH,
                 )
                 copy.start()
                 sent.append(copy)
         return sent
 
-    def arrived(source, where, slots, sems):
+    def arrived(source, where, these, slots, sems):
         pltpu.make_async_remote_copy(
-            source, slots.at[where], sems.at[0, 0], sems.at[1, where], device_id=plane[0], device_id_type=MESH
+            source.at[these, :], slots.at[where, these, :], sems.at[0, 0], sems.at[1, where],
+            device_id=plane[0], device_id_type=MESH,
         ).wait_recv()
 
-    sent = exchange(mine_ref.at[0], [(plane, spot, plane_ref, plane_sem)])
-    plane_ref[spot] = mine_ref[0]
+    sent = exchange(mine_ref.at[0], [(plane, spot, rows, plane_ref, plane_sem)])
+    plane_ref[spot, rows, :] = mine_ref[0, rows, :]
     for peer in plane:
-        arrived(mine_ref.at[0], XS * peer["board_0"] + peer["board_1"], plane_ref, plane_sem)
-    mine_ref[1] = functools.reduce(jnp.add, [plane_ref[k] for k in range(YS * XS)])
-    sent += exchange(mine_ref.at[1], [(line, z, line_ref, line_sem), (cross, z, cross_ref, cross_sem)])
-    line_ref[z] = mine_ref[1]
+        arrived(mine_ref.at[0], XS * peer["board_0"] + peer["board_1"], rows, plane_ref, plane_sem)
+    mine_ref[1, rows, :] = functools.reduce(jnp.add, [plane_ref[k, rows, :] for k in range(YS * XS)])
+    sent += exchange(
+        mine_ref.at[1], [(line, z, rows, line_ref, line_sem), (cross, z, ends_row, cross_ref, cross_sem)]
+    )
+    line_ref[z, rows, :] = mine_ref[1, rows, :]
     for peer in line:
-        arrived(mine_ref.at[1], peer["board_2"], line_ref, line_sem)
+        arrived(mine_ref.at[1], peer["board_2"], rows, line_ref, line_sem)
     for peer in cross:
-        arrived(mine_ref.at[1], peer["board_2"], cross_ref, cross_sem)
-    total = functools.reduce(jnp.add, [line_ref[k] for k in range(ZS)])
-    rest = functools.reduce(jnp.add, [cross_ref[k] for k in range(ZS)])
-    hand_ref[...] = total
-    ends = total[6:7] + rest[6:7]
-    ratio_ref[...] = ends[:, 0:1] / ends[:, 1:2]
+        arrived(mine_ref.at[1], peer["board_2"], ends_row, cross_ref, cross_sem)
+    total = functools.reduce(jnp.add, [line_ref[k, rows, :] for k in range(ZS)])
+    rest = functools.reduce(jnp.add, [cross_ref[k, ends_row, :] for k in range(ZS)])
+    hand_ref[rows, :] = total
+    hand_ref[lanes // 128 :, :] = jnp.zeros((8 - lanes // 128, 128), F32)
+    ends = total[ends_row] + rest
+    ratio_ref[...] = ends[:, 126:127] / ends[:, 127:128]
     for copy in sent:
         copy.wait_send()
 

time: 32.6 us -> 32.4 us (level)
  no operation moved by 1% of the time
where the time goes in v8:
time: 32.4 us; the launch traced here: 32.3 us
  Pallas kernels  31.6 us (98%)
  between operations  0.64 us (2%)
    pallas_call x1, Pallas kernels, local(): pl.pallas_call(functools.partial(fused_kernel, total_boards, hand_count),...  30.3 us
    pallas_call x1, Pallas kernels, write_out(): pl.pallas_call(write_kernel, out_shape=tuple((jax.ShapeDtypeStruct(a.shap...  1.37 us

profile of v8, /device:TPU:1, one launch (start us, length us, event | category | flops | bytes accessed | tf_op | source)
XLA Modules:
  0.0 32.3 jit_solution(16305412310243810194)
XLA Ops:
  0.6 30.3 %shard_map.85 = (f32[64,663]{1,0:T(8,128)S(1)}, f32[8,128]{1,0:T(8,128)S(1)}, f32[1,1]{1,0:T(1,128)}) custom-call(bf16[64,663]{1,0:T(8,128)(2,1)} %reach_hbm.1, s32[64,1326]{1,0:T(8,128)} %rank_hbm.1, s32[2,1326]{1,0:T(2,128)} %bitcast.6, f32[1,64]{1,0:T(1,128)} %bitcast.8, f32[1,64]{1,0:T(1,128)} %bitcast.9, f32[663]{0:T(1024)} %trav_hbm.1), custom_call_target="tpu_custom_call" | custom-call | flops 1000000000 | bytes 1000000 | tf_op jit(solution)/shard_map/pallas_call | solution.py:450
  30.9 1.4 %shard_map.86 = (f32[64,663]{1,0:T(8,128)}, f32[8,128]{1,0:T(8,128)}, f32[1,1]{1,0:T(1,128)}) custom-call(f32[64,663]{1,0:T(8,128)S(1)} %get-tuple-element.9.refs_0_, f32[8,128]{1,0:T(8,128)S(1)} %get-tuple-element.10.refs_1_, f32[1,1]{1,0:T(1,128)} %get-tuple-element.11.refs_2_), custom_call_target="tpu_custom_call" | custom-call | flops 1000000 | bytes 1000000 | tf_op jit(solution)/shard_map/pallas_call | solution.py:432

commit v9 on v8

--- a/solution.py
+++ b/solution.py
@@ -163,15 +163,16 @@
 
     digit = iota((16, lanes), 0).astype(F32).astype(BF16)
 
+    pair = (iota((16, lanes), 0) // GROUP).astype(F32).astype(BF16)
+
     def high_factor(half, g):
-        for b in range(GROUP):
-            at = GROUP * g + b
-            hi = jnp.broadcast_to(f_ref[0, at : at + 1, cols_of(half)], (16, lanes)).astype(BF16)
-            reach = jnp.broadcast_to(f_ref[2, at : at + 1, cols_of(half)], (16, lanes)).astype(BF16)
-            for part in range(HI // 16):
-                rows = slice(HI * b + 16 * part, HI * b + 16 * part + 16)
-                hit = hi == digit + BF16(16 * part)
-                a_ref[g, rows, cols_of(half)] = jnp.where(hit, reach, BF16(0))
+        boards_here = slice(GROUP * g, GROUP * (g + 1))
+        hi, reach = (
+            jnp.concatenate([f_ref[k, boards_here, cols_of(half)]] * 2, axis=0).astype(BF16) for k in (0, 2)
+        )
+        for two in range(HI // 2):
+            hit = hi == pair + BF16(2 * two)
+            a_ref[g, 16 * two : 16 * two + 16, cols_of(half)] = jnp.where(hit, reach, BF16(0))
 
     def low_factor(half, g):
         for b in range(GROUP):
@@ -244,8 +245,6 @@
         card_totals = card_totals + lax.dot_general(
             x_ref[0:boards, cols_of(half)], hold, NT, preferred_element_type=F32
         )
-    tabulate(0)
-    tabulate(1)
     wide = jnp.concatenate([card_totals, jnp.zeros((boards, 64), F32)], axis=1)
     pair_lanes = PARTS * CARDS * ROWS
     turned = jnp.transpose(q_ref[...].reshape(CARDS * ROWS, block))
@@ -266,14 +265,16 @@
 
     def lay_out(g):
         for t in range(tiles):
-            parts = [
-                jnp.where(
-                    upper,
-                    h_refs[g][pl.ds(4 * t + k, GROUP, stride=HI), :],
-                    h_refs[g][pl.ds(4 * t + k + GROUP * HI, GROUP, stride=HI), :],
+            parts = []
+            for k in range(4):
+                at = GROUP * (4 * t + k)
+                parts.append(
+                    jnp.where(
+                        upper,
+                        h_refs[g][at : at + GROUP, :],
+                        h_refs[g][GROUP * HI + at : GROUP * HI + at + GROUP, :],
+                    )
                 )
-                for k in range(4)
-            ]
             row = None
             for k in range(4):
                 moved = parts[(3 + k) % 4]
@@ -320,7 +321,7 @@
     stages = (tabulate, lay_out, add_rows, look_up)
     for step in range(groups + len(stages) - 1):
         for k, stage in enumerate(stages):
-            if 0 <= step - k < groups and (k or step > 1):
+            if 0 <= step - k < groups:
                 stage(step - k)
     sum_copy = to_partner(s_ref.at[1 - me], s_ref.at[2], sum_sem)
 

time: 32.4 us -> 32.3 us (level)
  no operation moved by 1% of the time
where the time goes in v9:
time: 32.3 us; the launch traced here: 32.1 us
  Pallas kernels  31.4 us (97%)
  between operations  0.64 us (2%)
    pallas_call x1, Pallas kernels, local(): pl.pallas_call(functools.partial(fused_kernel, total_boards, hand_count),...  30.1 us
    pallas_call x1, Pallas kernels, write_out(): pl.pallas_call(write_kernel, out_shape=tuple((jax.ShapeDtypeStruct(a.shap...  1.37 us

profile of v9, /device:TPU:1, one launch (start us, length us, event | category | flops | bytes accessed | tf_op | source)
XLA Modules:
  0.0 32.1 jit_solution(5346551546679313719)
XLA Ops:
  0.6 30.1 %shard_map.85 = (f32[64,663]{1,0:T(8,128)S(1)}, f32[8,128]{1,0:T(8,128)S(1)}, f32[1,1]{1,0:T(1,128)}) custom-call(bf16[64,663]{1,0:T(8,128)(2,1)} %reach_hbm.1, s32[64,1326]{1,0:T(8,128)} %rank_hbm.1, s32[2,1326]{1,0:T(2,128)} %bitcast.6, f32[1,64]{1,0:T(1,128)} %bitcast.8, f32[1,64]{1,0:T(1,128)} %bitcast.9, f32[663]{0:T(1024)} %trav_hbm.1), custom_call_target="tpu_custom_call" | custom-call | flops 1000000000 | bytes 1000000 | tf_op jit(solution)/shard_map/pallas_call | solution.py:451
  30.7 1.4 %shard_map.86 = (f32[64,663]{1,0:T(8,128)}, f32[8,128]{1,0:T(8,128)}, f32[1,1]{1,0:T(1,128)}) custom-call(f32[64,663]{1,0:T(8,128)S(1)} %get-tuple-element.9.refs_0_, f32[8,128]{1,0:T(8,128)S(1)} %get-tuple-element.10.refs_1_, f32[1,1]{1,0:T(1,128)} %get-tuple-element.11.refs_2_), custom_call_target="tpu_custom_call" | custom-call | flops 1000000 | bytes 1000000 | tf_op jit(solution)/shard_map/pallas_call | solution.py:433

commit v10 on v9

--- a/solution.py
+++ b/solution.py
@@ -20,7 +20,6 @@
 SLOT = 32
 GROUP = 8
 DBLOCK = 4
-WRITES = 4
 YS, XS, ZS = 4, 4, 8
 MESH = pl.DeviceIdType.MESH
 NT = (((1,), (1,)), ((), ()))
@@ -61,7 +60,7 @@
 def fused_kernel(
     total_boards, hand_count,
     reach_hbm, rank_hbm, cards_hbm, pot_hbm, bet_hbm, trav_hbm,
-    values_ref, hand_ref, ratio_ref,
+    values_ref, hand_ref,
     reach_ref, rank_ref, cards_ref, pot_ref, bet_ref, trav_ref, io_sem,
     x_ref, p_ref, o_ref, w_ref, g_ref, q_ref, l_ref, f_ref, a_ref, b_ref, h0_ref, h1_ref, h2_ref, h3_ref, t0_ref, t1_ref, t2_ref, t3_ref, s_ref, c_ref,
     swap_ref, mine_ref, plane_ref, line_ref, cross_ref,
@@ -408,21 +407,16 @@
     total = functools.reduce(jnp.add, [line_ref[k, rows, :] for k in range(ZS)])
     rest = functools.reduce(jnp.add, [cross_ref[k, ends_row, :] for k in range(ZS)])
     hand_ref[rows, :] = total
-    hand_ref[lanes // 128 :, :] = jnp.zeros((8 - lanes // 128, 128), F32)
     ends = total[ends_row] + rest
-    ratio_ref[...] = ends[:, 126:127] / ends[:, 127:128]
+    hand_ref[lanes // 128 :, :] = jnp.broadcast_to(ends / pltpu.roll(ends, 127, 1), (8 - lanes // 128, 128))
     for copy in sent:
         copy.wait_send()
 
 
-def write_kernel(*refs):
-    count = (len(refs) - 1) // 2
-    pieces = []
-    for source, target in zip(refs[:count], refs[count:-1]):
-        step = max(source.shape[0] // WRITES // 8 * 8, min(source.shape[0], 8))
-        for start in range(0, source.shape[0], step):
-            pieces.append((source.at[start : start + step, :], target.at[start : start + step, :]))
-    copies = [pltpu.make_async_copy(*piece, refs[-1].at[k]) for k, piece in enumerate(pieces)]
+def write_kernel(values_ref, hand_ref, values_out, hand_out, ratio_out, ratio_ref, sems):
+    ratio_ref[...] = hand_ref[7:8, 126:127]
+    moves = ((values_ref, values_out), (hand_ref, hand_out), (ratio_ref, ratio_out))
+    copies = [pltpu.make_async_copy(source, target, sems.at[k]) for k, (source, target) in enumerate(moves)]
     for copy in copies:
         copy.start()
     for copy in copies:
@@ -430,12 +424,13 @@
 
 
 def write_out(*arrays):
+    shapes = [a.shape for a in arrays] + [(1, 1)]
     return pl.pallas_call(
         write_kernel,
-        out_shape=tuple(jax.ShapeDtypeStruct(a.shape, a.dtype) for a in arrays),
+        out_shape=tuple(jax.ShapeDtypeStruct(shape, F32) for shape in shapes),
         in_specs=[pl.BlockSpec(memory_space=pltpu.VMEM)] * len(arrays),
-        out_specs=(pl.BlockSpec(memory_space=pl.ANY),) * len(arrays),
-        scratch_shapes=[pltpu.SemaphoreType.DMA((WRITES + len(arrays),))],
+        out_specs=(pl.BlockSpec(memory_space=pl.ANY),) * len(shapes),
+        scratch_shapes=[pltpu.VMEM((1, 1), F32), pltpu.SemaphoreType.DMA((len(shapes),))],
         cost_estimate=pl.CostEstimate(flops=10**6, bytes_accessed=10**6, transcendentals=0),
     )(*(pltpu.with_memory_space_constraint(a, pltpu.VMEM) for a in arrays))
 
@@ -448,15 +443,14 @@
     half = boards // 2
     total_boards = boards * lax.axis_size(BOARD)
     whole = pl.BlockSpec(memory_space=pltpu.VMEM)
-    board_values, hand_rows, ratio = pl.pallas_call(
+    board_values, hand_rows = pl.pallas_call(
         functools.partial(fused_kernel, total_boards, hand_count),
         out_shape=(
             pltpu.VMEM((boards, own_count), F32),
             pltpu.VMEM((8, 128), F32),
-            pltpu.VMEM((1, 1), F32),
         ),
         in_specs=[pl.BlockSpec(memory_space=pl.ANY)] * 6,
-        out_specs=(whole, whole, whole),
+        out_specs=(whole, whole),
         scratch_shapes=[
             pltpu.VMEM((boards, own_count), BF16),
             pltpu.VMEM((half, hand_count), jnp.int32),
@@ -496,7 +490,7 @@
         ),
         cost_estimate=pl.CostEstimate(flops=10**9, bytes_accessed=10**6, transcendentals=0),
     )(opp_reach, hand_rank, hand_cards.T, pot[None, :], bet_frac[None, :], trav_reach)
-    board_values, hand_rows, ratio = write_out(board_values, hand_rows, ratio)
+    board_values, hand_rows, ratio = write_out(board_values, hand_rows)
     return board_values, hand_rows.reshape(-1)[:own_count], ratio[0, 0]
 
 

time: 32.3 us -> 31 us (0.960)
  Pallas kernels: 31.4 us -> 30.2 us
    pallas_call x1, Pallas kernels: 1.37 us -> 0.71 us  [write_out(): pl.pallas_call(write_kernel, out_shape=tuple((jax.ShapeDtypeStruct(shape,...]
    pallas_call x1, Pallas kernels: 30.1 us -> 29.5 us  [local(): pl.pallas_call(functools.partial(fused_kernel, total_boards, hand_count),...]
where the time goes in v10:
time: 31 us; the launch traced here: 30.8 us
  Pallas kernels  30.2 us (97%)
  between operations  0.64 us (2%)
    pallas_call x1, Pallas kernels, local(): pl.pallas_call(functools.partial(fused_kernel, total_boards, hand_count),...  29.5 us
    pallas_call x1, Pallas kernels, write_out(): pl.pallas_call(write_kernel, out_shape=tuple((jax.ShapeDtypeStruct(shape,...  0.71 us

profile of v10, /device:TPU:1, one launch (start us, length us, event | category | flops | bytes accessed | tf_op | source)
XLA Modules:
  0.0 30.8 jit_solution(2799027511569196749)
XLA Ops:
  0.6 29.5 %shard_map.85 = (f32[64,663]{1,0:T(8,128)S(1)}, f32[8,128]{1,0:T(8,128)S(1)}) custom-call(bf16[64,663]{1,0:T(8,128)(2,1)} %reach_hbm.1, s32[64,1326]{1,0:T(8,128)} %rank_hbm.1, s32[2,1326]{1,0:T(2,128)} %bitcast.6, f32[1,64]{1,0:T(1,128)} %bitcast.8, f32[1,64]{1,0:T(1,128)} %bitcast.9, f32[663]{0:T(1024)} %trav_hbm.1), custom_call_target="tpu_custom_call" | custom-call | flops 1000000000 | bytes 1000000 | tf_op jit(solution)/shard_map/pallas_call | solution.py:446
  30.1 0.7 %shard_map.86 = (f32[64,663]{1,0:T(8,128)}, f32[8,128]{1,0:T(8,128)}, f32[1,1]{1,0:T(1,128)}) custom-call(f32[64,663]{1,0:T(8,128)S(1)} %get-tuple-element.8.values_ref, f32[8,128]{1,0:T(8,128)S(1)} %get-tuple-element.9.hand_ref), custom_call_target="tpu_custom_call" | custom-call | flops 1000000 | bytes 1000000 | tf_op jit(solution)/shard_map/pallas_call | solution.py:428

commit v11 on v10

--- a/solution.py
+++ b/solution.py
@@ -325,6 +325,8 @@
     sum_copy = to_partner(s_ref.at[1 - me], s_ref.at[2], sum_sem)
 
     pair_copy.wait()
+    for load in loads[4:]:
+        load.wait()
     for g in range(groups):
         look_up(g, me)
     back = [p_ref[:, q, :, cols_of(me)].reshape(CARDS * ROWS, lanes) for q in range(PARTS)]
@@ -336,32 +338,31 @@
     held = jnp.dot(
         l_ref[:, :, pair_lanes:].reshape(4 * boards, 128)[:, 0:64], hold, preferred_element_type=F32
     )
-    sum_copy.wait()
-    for load in loads[4:]:
-        load.wait()
-    part = mass = None
-    for k, core in ((0, me), (1, 1 - me)):
+    trav = trav_ref[...].reshape(1, own_count)
+
+    def ready(k, core):
         at = 2 * boards * k
         live = (
             0.5 * jnp.sum(l_ref[k, :, pair_lanes:].astype(F32).reshape(2, boards, 128).sum(0), axis=1, keepdims=True)
             - (held[at : at + boards] + held[at + boards : at + 2 * boards])
         )[:, 0:own_count] + reach_ref[rows_of(core), :].astype(F32)
-        sums = s_ref[me] if k == 0 else s_ref[2]
-        margin = (sums - (shared[at : at + boards] + shared[at + boards : at + 2 * boards]))[:, 0:own_count]
         pot = column(pot_ref[...], core * boards, boards)
-        bet = column(bet_ref[...], core * boards, boards)
-        half_pot = 0.5 * pot
-        half_pot, bet = half_pot / hand_count, bet / hand_count
-        stake = half_pot * live
-        values = jnp.maximum((half_pot + bet * pot) * margin, -stake)
+        bet = column(bet_ref[...], core * boards, boards) / hand_count
+        half_pot = 0.5 * pot / hand_count
+        return half_pot + bet * pot, shared[at : at + boards] + shared[at + boards : at + 2 * boards], half_pot * live
+
+    def settle(core, sums, rate, taken, stake):
+        values = jnp.maximum(rate * (sums - taken)[:, 0:own_count], -stake)
         values_ref[rows_of(core), :] = values
-        values, stake = (jnp.sum(v, axis=0, keepdims=True) for v in (values, stake))
-        part = values if part is None else part + values
-        mass = stake if mass is None else mass + stake
-    part, mass = part / total_boards, mass / total_boards
-    trav = trav_ref[...].reshape(1, own_count)
+        return jnp.sum(values, axis=0, keepdims=True)
+
+    here, there = ready(0, me), ready(1, 1 - me)
+    mass = (jnp.sum(here[2], axis=0, keepdims=True) + jnp.sum(there[2], axis=0, keepdims=True)) / total_boards
+    denominator = jnp.sum(mass * trav, axis=1, keepdims=True)
+    part = settle(me, s_ref[me], *here)
+    sum_copy.wait()
+    part = (part + settle(1 - me, s_ref[2], *there)) / total_boards
     numerator = jnp.sum(part * trav, axis=1, keepdims=True)
-    denominator = jnp.sum(mass * trav, axis=1, keepdims=True)
 
     spot = XS * y + x
     last = lanes // 128 - 1

time: 31 us -> 30.8 us (level)
  no operation moved by 1% of the time
where the time goes in v11:
time: 30.8 us; the launch traced here: 30.7 us
  Pallas kernels  30 us (97%)
  between operations  0.64 us (2%)
    pallas_call x1, Pallas kernels, local(): pl.pallas_call(functools.partial(fused_kernel, total_boards, hand_count),...  29.3 us
    pallas_call x1, Pallas kernels, write_out(): pl.pallas_call(write_kernel, out_shape=tuple((jax.ShapeDtypeStruct(shape,...  0.71 us

profile of v11, /device:TPU:1, one launch (start us, length us, event | category | flops | bytes accessed | tf_op | source)
XLA Modules:
  0.0 30.7 jit_solution(5365700303229579256)
XLA Ops:
  0.6 29.3 %shard_map.85 = (f32[64,663]{1,0:T(8,128)S(1)}, f32[8,128]{1,0:T(8,128)S(1)}) custom-call(bf16[64,663]{1,0:T(8,128)(2,1)} %reach_hbm.1, s32[64,1326]{1,0:T(8,128)} %rank_hbm.1, s32[2,1326]{1,0:T(2,128)} %bitcast.6, f32[1,64]{1,0:T(1,128)} %bitcast.8, f32[1,64]{1,0:T(1,128)} %bitcast.9, f32[663]{0:T(1024)} %trav_hbm.1), custom_call_target="tpu_custom_call" | custom-call | flops 1000000000 | bytes 1000000 | tf_op jit(solution)/shard_map/pallas_call | solution.py:447
  30.0 0.7 %shard_map.86 = (f32[64,663]{1,0:T(8,128)}, f32[8,128]{1,0:T(8,128)}, f32[1,1]{1,0:T(1,128)}) custom-call(f32[64,663]{1,0:T(8,128)S(1)} %get-tuple-element.8.values_ref, f32[8,128]{1,0:T(8,128)S(1)} %get-tuple-element.9.hand_ref), custom_call_target="tpu_custom_call" | custom-call | flops 1000000 | bytes 1000000 | tf_op jit(solution)/shard_map/pallas_call | solution.py:429

commit v12 on v11

--- a/solution.py
+++ b/solution.py
@@ -365,14 +365,14 @@
     numerator = jnp.sum(part * trav, axis=1, keepdims=True)
 
     spot = XS * y + x
-    last = lanes // 128 - 1
-    for k in range(last):
-        mine_ref[0, k : k + 1, :] = part[:, 128 * k : 128 * (k + 1)]
-    fill = jnp.concatenate([part[:, 128 * last :], jnp.zeros((1, lanes - own_count), F32)], axis=1)
-    lane = iota((1, 128), 1)
-    mine_ref[0, last : last + 1, :] = jnp.where(lane == 126, numerator, jnp.where(lane == 127, denominator, fill))
-
-    rows, ends_row = slice(0, lanes // 128), slice(last, last + 1)
+    for k in range(lanes // 128):
+        size = min(128, own_count - 128 * k)
+        mine_ref[0, k : k + 1, 0:size] = part[:, 128 * k : 128 * k + size]
+        if size < 128:
+            mine_ref[0, k : k + 1, size:] = jnp.zeros((1, 128 - size), F32)
+    mine_ref[0, 6:7, :] = jnp.broadcast_to(numerator, (1, 128))
+    mine_ref[0, 7:8, :] = jnp.broadcast_to(denominator, (1, 128))
+    rows, ends_row = slice(0, 8), slice(6, 8)
 
     def exchange(source, groups):
         sent = []
@@ -407,15 +407,15 @@
         arrived(mine_ref.at[1], peer["board_2"], ends_row, cross_ref, cross_sem)
     total = functools.reduce(jnp.add, [line_ref[k, rows, :] for k in range(ZS)])
     rest = functools.reduce(jnp.add, [cross_ref[k, ends_row, :] for k in range(ZS)])
-    hand_ref[rows, :] = total
-    ends = total[ends_row] + rest
-    hand_ref[lanes // 128 :, :] = jnp.broadcast_to(ends / pltpu.roll(ends, 127, 1), (8 - lanes // 128, 128))
+    hand_ref[0:7, :] = total[0:7]
+    ends = total[6:8] + rest
+    hand_ref[7:8, :] = ends[0:1] / ends[1:2]
     for copy in sent:
         copy.wait_send()
 
 
 def write_kernel(values_ref, hand_ref, values_out, hand_out, ratio_out, ratio_ref, sems):
-    ratio_ref[...] = hand_ref[7:8, 126:127]
+    ratio_ref[...] = hand_ref[7:8, 0:1]
     moves = ((values_ref, values_out), (hand_ref, hand_out), (ratio_ref, ratio_out))
     copies = [pltpu.make_async_copy(source, target, sems.at[k]) for k, (source, target) in enumerate(moves)]
     for copy in copies:

time: 30.8 us -> 30.8 us (level)
  no operation moved by 1% of the time
where the time goes in v12:
time: 30.8 us; the launch traced here: 30.6 us
  Pallas kernels  30 us (97%)
  between operations  0.64 us (2%)
    pallas_call x1, Pallas kernels, local(): pl.pallas_call(functools.partial(fused_kernel, total_boards, hand_count),...  29.3 us
    pallas_call x1, Pallas kernels, write_out(): pl.pallas_call(write_kernel, out_shape=tuple((jax.ShapeDtypeStruct(shape,...  0.71 us

profile of v12, /device:TPU:1, one launch (start us, length us, event | category | flops | bytes accessed | tf_op | source)
XLA Modules:
  0.0 30.6 jit_solution(12544090081564795581)
XLA Ops:
  0.6 29.3 %shard_map.85 = (f32[64,663]{1,0:T(8,128)S(1)}, f32[8,128]{1,0:T(8,128)S(1)}) custom-call(bf16[64,663]{1,0:T(8,128)(2,1)} %reach_hbm.1, s32[64,1326]{1,0:T(8,128)} %rank_hbm.1, s32[2,1326]{1,0:T(2,128)} %bitcast.6, f32[1,64]{1,0:T(1,128)} %bitcast.8, f32[1,64]{1,0:T(1,128)} %bitcast.9, f32[663]{0:T(1024)} %trav_hbm.1), custom_call_target="tpu_custom_call" | custom-call | flops 1000000000 | bytes 1000000 | tf_op jit(solution)/shard_map/pallas_call | solution.py:447
  29.9 0.7 %shard_map.86 = (f32[64,663]{1,0:T(8,128)}, f32[8,128]{1,0:T(8,128)}, f32[1,1]{1,0:T(1,128)}) custom-call(f32[64,663]{1,0:T(8,128)S(1)} %get-tuple-element.8.values_ref, f32[8,128]{1,0:T(8,128)S(1)} %get-tuple-element.9.hand_ref), custom_call_target="tpu_custom_call" | custom-call | flops 1000000 | bytes 1000000 | tf_op jit(solution)/shard_map/pallas_call | solution.py:429

commit v13 on v12

--- a/solution.py
+++ b/solution.py
@@ -209,6 +209,13 @@
         tabulate(g, me)
     swap.wait()
     place(1 - me, swap_ref[...])
+    card = iota((64, lanes), 0).astype(F32)
+    card_totals = jnp.zeros((boards, 64), F32)
+    for half in (1 - me, me):
+        hold = ((card == c_ref[0:1, cols_of(half)]) | (card == c_ref[1:2, cols_of(half)])).astype(F32).astype(BF16)
+        card_totals = card_totals + lax.dot_general(
+            x_ref[0:boards, cols_of(half)], hold, NT, preferred_element_type=F32
+        )
     to_cards(1 - me, True)
 
     part_of = iota((ROWS, block), 1) // boards
@@ -237,13 +244,6 @@
         return carry
 
     lax.fori_loop(0, CARDS // DBLOCK, pairs, 0)
-    card = iota((64, lanes), 0).astype(F32)
-    card_totals = jnp.zeros((boards, 64), F32)
-    for half in (1 - me, me):
-        hold = ((card == c_ref[0:1, cols_of(half)]) | (card == c_ref[1:2, cols_of(half)])).astype(F32).astype(BF16)
-        card_totals = card_totals + lax.dot_general(
-            x_ref[0:boards, cols_of(half)], hold, NT, preferred_element_type=F32
-        )
     wide = jnp.concatenate([card_totals, jnp.zeros((boards, 64), F32)], axis=1)
     pair_lanes = PARTS * CARDS * ROWS
     turned = jnp.transpose(q_ref[...].reshape(CARDS * ROWS, block))

time: 30.8 us -> 30.9 us (level)
  no operation moved by 1% of the time
where the time goes in v13:
time: 30.9 us; the launch traced here: 30.8 us
  Pallas kernels  30.1 us (97%)
  between operations  0.64 us (2%)
    pallas_call x1, Pallas kernels, local(): pl.pallas_call(functools.partial(fused_kernel, total_boards, hand_count),...  29.4 us
    pallas_call x1, Pallas kernels, write_out(): pl.pallas_call(write_kernel, out_shape=tuple((jax.ShapeDtypeStruct(shape,...  0.71 us

profile of v13, /device:TPU:1, one launch (start us, length us, event | category | flops | bytes accessed | tf_op | source)
XLA Modules:
  0.0 30.8 jit_solution(4998369241688298304)
XLA Ops:
  0.6 29.4 %shard_map.85 = (f32[64,663]{1,0:T(8,128)S(1)}, f32[8,128]{1,0:T(8,128)S(1)}) custom-call(bf16[64,663]{1,0:T(8,128)(2,1)} %reach_hbm.1, s32[64,1326]{1,0:T(8,128)} %rank_hbm.1, s32[2,1326]{1,0:T(2,128)} %bitcast.6, f32[1,64]{1,0:T(1,128)} %bitcast.8, f32[1,64]{1,0:T(1,128)} %bitcast.9, f32[663]{0:T(1024)} %trav_hbm.1), custom_call_target="tpu_custom_call" | custom-call | flops 1000000000 | bytes 1000000 | tf_op jit(solution)/shard_map/pallas_call | solution.py:447
  30.0 0.7 %shard_map.86 = (f32[64,663]{1,0:T(8,128)}, f32[8,128]{1,0:T(8,128)}, f32[1,1]{1,0:T(1,128)}) custom-call(f32[64,663]{1,0:T(8,128)S(1)} %get-tuple-element.8.values_ref, f32[8,128]{1,0:T(8,128)S(1)} %get-tuple-element.9.hand_ref), custom_call_target="tpu_custom_call" | custom-call | flops 1000000 | bytes 1000000 | tf_op jit(solution)/shard_map/pallas_call | solution.py:429
